TPU v7x, 256 devices: a 2x2x32 block of a 4x8x32 slice. The times are simulated.
256 devices in a mesh: ga: 4 (over y, x), row: 32 (over z), col: 2 (over core).
Axes of the slice: x: 2, y: 2, z: 32, core: 2. Of those that a mesh axis runs over, the one named last changes fastest.
The devices are a block of a 4x8x32 slice.
Arguments:
- pair: bfloat16 [2048, 512, 128], P(('ga', 'row', 'col')), parts along dimension 0, may hold values from -480 to 480
- residue_mask: int32 [2048], P('ga'), parts along dimension 0, may hold values from 0 to 1, as said below
- targets: int32 [2048, 512], P(('ga', 'row', 'col')), parts along dimension 0, may hold values from 0 to 63
- ln_gain: float32 [2, 128], replicated, may hold values from 0.25 to 1.75
- ln_shift: float32 [2, 128], replicated, may hold values from -3 to 3
- w_in: bfloat16 [5, 128, 128], P(None, None, 'col'), may hold values from -0.5 to 0.5
- b_in: float32 [5, 128], replicated, may hold values from -3 to 3
- w_out: bfloat16 [128, 128], P('col'), may hold values from -0.5 to 0.5
- b_out: float32 [128], replicated, may hold values from -3 to 3
- head_weight: bfloat16 [128, 64], replicated, may hold values from -0.5 to 0.5
- head_bias: float32 [64], replicated, may hold values from -4 to 4
Outputs:
- update: bfloat16 [2048, 512, 128], P(('ga', 'row', 'col')), parts along dimension 0
- pair_loss: float32 [2048, 512], P(('ga', 'row', 'col')), parts along dimension 0
There are 4 independent parts, one for each index of `ga`. A program takes and returns all parts, laid end to end along the dimension named above; an argument that names none is the same for every part. Nothing has to cross between parts.
Inputs may be any that keep to these rules, and one draw needn't show every extreme that they name: `residue_mask`: each part's entries are 1 for residues 0 to some length - 1 and 0 after it; the length is at least 256 and at most 512.
All inputs are finite; a program needn't handle non-finite values.
Results may differ from a plain program's by a relative error of at most 0.0055.
Values may be sent and summed in bfloat16 or wider, within the bound.
No kernel may reach another device: no remote copies, remote signals or barrier semaphores. Data moves between devices by JAX's collectives and lax.ppermute only.
A program may use at most 64 MiB of HBM per device.

v0:
```python
import jax
import jax.numpy as jnp
from jax import lax
from jax.sharding import PartitionSpec as P


def normalize(values, gain_vec, shift_vec, epsilon, reduce_axis):
    average = jnp.mean(values, axis=reduce_axis, keepdims=True)
    centred = values - average
    spread = jnp.mean(centred * centred, axis=reduce_axis, keepdims=True)
    return centred * lax.rsqrt(spread + epsilon) * gain_vec + shift_vec


def local(
    pair, residue_mask, targets, ln_gain, ln_shift, w_in, b_in, w_out, b_out, head_weight, head_bias
):
    row_count, length, pair_width = pair.shape
    groups = lax.axis_size(("row", "col"))
    chan_share = pair_width // groups
    res_mask = residue_mask.astype(jnp.float32)
    own_mask = lax.dynamic_slice_in_dim(
        res_mask, lax.axis_index(("row", "col")) * row_count, row_count
    )
    pair_mask = own_mask[:, None] * res_mask[None, :]
    normed = normalize(pair.astype(jnp.float32), ln_gain[0], ln_shift[0], 0.1, -1).astype(
        jnp.bfloat16
    )
    projected = jnp.einsum(
        "ikc,ncd->ndik",
        normed,
        lax.all_gather(w_in, "col", axis=2, tiled=True),
        preferred_element_type=jnp.float32,
    )
    projected = projected + b_in[:, :, None, None]
    left_side = pair_mask * jax.nn.sigmoid(projected[1]) * projected[0]
    right_side = pair_mask * jax.nn.sigmoid(projected[3]) * projected[2]
    stacked = jnp.stack([left_side, right_side, projected[4]])
    left_side = stacked[0].astype(jnp.bfloat16)
    right_side = stacked[1].astype(jnp.bfloat16)
    gate_pre = stacked[2]
    row_devices = lax.axis_size("row")
    col_devices = lax.axis_size("col")
    left_blocks = left_side.reshape(row_devices, col_devices, chan_share, 1, row_count, length)
    right_blocks = right_side.reshape(row_devices, col_devices, chan_share, 1, row_count, length)
    moved = (
        lax.all_to_all(
            lax.all_to_all(left_blocks, "col", split_axis=1, concat_axis=4, tiled=True),
            "row",
            split_axis=0,
            concat_axis=3,
            tiled=True,
        ),
        lax.all_to_all(
            lax.all_to_all(right_blocks, "col", split_axis=1, concat_axis=4, tiled=True),
            "row",
            split_axis=0,
            concat_axis=3,
            tiled=True,
        ),
    )
    left_full = moved[0].reshape(chan_share, length, length)
    right_full = moved[1].reshape(chan_share, length, length)
    product = jnp.einsum("cik,cjk->cij", left_full, right_full, preferred_element_type=jnp.float32)
    product = product.astype(jnp.bfloat16).reshape(
        1, 1, chan_share, row_devices, col_devices * row_count, length
    )
    returned = lax.all_to_all(
        lax.all_to_all(product, "col", split_axis=4, concat_axis=1, tiled=True),
        "row",
        split_axis=3,
        concat_axis=0,
        tiled=True,
    )
    outer_prod = returned.reshape(pair_width, row_count, length)
    normed_outer = normalize(
        outer_prod.astype(jnp.float32),
        ln_gain[1][:, None, None],
        ln_shift[1][:, None, None],
        1.0,
        0,
    ).astype(jnp.bfloat16)
    mixed = jnp.einsum(
        "cij,cd->dij",
        normed_outer,
        lax.all_gather(w_out, "col", axis=0, tiled=True),
        preferred_element_type=jnp.float32,
    )
    update_chan = jax.nn.sigmoid(gate_pre) * (mixed + b_out[:, None, None])
    update = jnp.transpose(update_chan, (1, 2, 0)).astype(jnp.bfloat16)
    new_pair = (pair.astype(jnp.float32) + update.astype(jnp.float32)).astype(jnp.bfloat16)
    logits = (
        jnp.einsum("ijc,cb->ijb", new_pair, head_weight, preferred_element_type=jnp.float32)
        + head_bias
    )
    mirrored = lax.all_to_all(
        logits.astype(jnp.bfloat16), ("row", "col"), split_axis=1, concat_axis=0, tiled=True
    ).astype(logits.dtype)
    symmetric = logits + jnp.transpose(mirrored, (1, 0, 2))
    row_top = jnp.max(symmetric, axis=-1, keepdims=True)
    log_total = row_top[..., 0] + jnp.log(jnp.sum(jnp.exp(symmetric - row_top), axis=-1))
    bin_index = jnp.arange(symmetric.shape[2], dtype=jnp.int32)
    picked = jnp.sum(jnp.where(targets[..., None] == bin_index, symmetric, 0.0), axis=-1)
    pair_loss = pair_mask * (log_total - picked)
    return (update, pair_loss)


def solution(mesh):
    placed = (
        P(("ga", "row", "col"), None, None),
        P("ga"),
        P(("ga", "row", "col"), None),
        P(),
        P(),
        P(None, None, "col"),
        P(),
        P("col", None),
        P(),
        P(),
        P(),
    )
    return jax.shard_map(
        local,
        mesh=mesh,
        in_specs=placed,
        out_specs=(P(("ga", "row", "col"), None, None), P(("ga", "row", "col"), None)),
        check_vma=False,
    )
```

profile of v0, /device:TPU:37, one launch (start us, length us, event | category | flops | bytes accessed | tf_op | source)
XLA Modules:
  0.0 505.1 jit_solution(7631913060883814611)
XLA Ops:
  0.7 1.5 copy.51
  2.7 22.0 %all_gather.6 = bf16[5,128,128]{1,2,0:T(8,128)(2,1)S(1)} all-gather(bf16[5,128,64]{1,2,0:T(8,128)(2,1)S(1)} %copy-done.3), channel_id=1, replica_groups=mesh['ga'=4,'row'=32,'col'=2] {'col'}, dimensions={2}, use_global_device_ids=true | all-gather | bytes 245760 | tf_op jit(solution)/shard_map/all_gather | solution.py:31
  24.8 1.9 add_bitcast_fusion
  26.7 4.6 fusion.9
  31.3 1.8 copy-done.1
  33.1 2.5 squeeze.9
  35.6 3.5 div.51
  39.3 3.5 squeeze.8
  42.8 3.5 div.49
  46.2 8.3 %fusion.24 = (bf16[32,2,2,1,8,512]{5,4,2,0,3,1:T(8,128)(2,1)}, bf16[32,2,2,1,8,512]{5,4,2,0,3,1:T(8,128)(2,1)S(1)}) fusion(f32[32,2,2,1,8,512]{5,2,1,0,4,3:T(2,128)S(1)} %squeeze.9, f32[32,2,2,1,8,512]{5,2,1,0,4,3:T(2,128)} %div.51, f32[8,512]{1,0:T(8,128)S(1)} %broadcast_multiply_fusion, f32[32,2,2,1,8,512]{5,2,1,0,4,3:T(2,128)} %squeeze.8, ...), kind=kLoop, calls=%fused_computation.36 | loop fusion | flops 3145728 | bytes 10502144 | tf_op jit(solution)/shard_map/convert_element_type | solution.py:39
  54.5 4.6 all_to_all.102
  59.1 4.1 all-to-all-start.2
  63.2 1.1 copy.103
  65.0 13.4 %all-to-all-start.1 = ((bf16[32,1,2,1,16,512]{5,4,2,3,1,0:T(8,128)(2,1)}), bf16[32,1,2,1,16,512]{5,4,2,3,1,0:T(8,128)(2,1)S(1)}, u32[]{:S(2)}, u32[]{:S(2)}) async-start(bf16[32,1,2,1,16,512]{5,4,2,3,1,0:T(8,128)(2,1)} %bitcast.137), calls=%async_computation.1 | async-start | bytes 2097152 | tf_op jit(solution)/shard_map/all_to_all | solution.py:46
  78.4 1.2 copy.102
  79.5 103.5 %all-to-all-done.1 = bf16[32,1,2,1,16,512]{5,4,2,3,1,0:T(8,128)(2,1)S(1)} async-done(((bf16[32,1,2,1,16,512]{5,4,2,3,1,0:T(8,128)(2,1)}), bf16[32,1,2,1,16,512]{5,4,2,3,1,0:T(8,128)(2,1)S(1)}, u32[]{:S(2)}, u32[]{:S(2)}) %all-to-all-start.1) | async-done | bytes 1048608 | tf_op jit(solution)/shard_map/all_to_all | solution.py:46
  183.0 8.0 %all-to-all-start.3 = ((bf16[32,1,2,1,16,512]{5,4,2,3,1,0:T(8,128)(2,1)}), bf16[32,1,2,1,16,512]{5,4,2,3,1,0:T(8,128)(2,1)S(1)}, u32[]{:S(2)}, u32[]{:S(2)}) async-start(bf16[32,1,2,1,16,512]{5,4,2,3,1,0:T(8,128)(2,1)} %bitcast.138), calls=%async_computation.3 | async-start | bytes 2097152 | tf_op jit(solution)/shard_map/all_to_all | solution.py:53
  192.1 103.4 %all-to-all-done.3 = bf16[32,1,2,1,16,512]{5,4,2,3,1,0:T(8,128)(2,1)S(1)} async-done(((bf16[32,1,2,1,16,512]{5,4,2,3,1,0:T(8,128)(2,1)}), bf16[32,1,2,1,16,512]{5,4,2,3,1,0:T(8,128)(2,1)S(1)}, u32[]{:S(2)}, u32[]{:S(2)}) %all-to-all-start.3) | async-done | bytes 1048608 | tf_op jit(solution)/shard_map/all_to_all | solution.py:53
  296.9 5.1 %all_to_all.103 = bf16[1,1,2,32,16,512]{5,3,2,1,0,4:T(8,128)(2,1)S(1)} all-to-all(bf16[1,1,2,32,16,512]{5,3,2,1,0,4:T(8,128)(2,1)S(1)} %copy.63), channel_id=1, replica_groups=mesh['ga'=4,'row'=32,'col'=2] {'col'}, dimensions={4} | all-to-all | bytes 2097152 | tf_op jit(solution)/shard_map/all_to_all | solution.py:68
  303.7 7.9 %all-to-all-start.5 = ((bf16[1,2,2,32,8,512]{5,4,1,2,0,3:T(8,128)(2,1)}), bf16[1,2,2,32,8,512]{5,4,1,2,0,3:T(8,128)(2,1)S(1)}, u32[]{:S(2)}, u32[]{:S(2)}) async-start(bf16[1,2,2,32,8,512]{5,4,1,2,0,3:T(8,128)(2,1)} %copy.65), calls=%async_computation.5 | async-start | bytes 2097152 | tf_op jit(solution)/shard_map/all_to_all | solution.py:67
  311.5 2.2 all_gather.7
  313.7 102.5 %all-to-all-done.5 = bf16[1,2,2,32,8,512]{5,4,1,2,0,3:T(8,128)(2,1)S(1)} async-done(((bf16[1,2,2,32,8,512]{5,4,1,2,0,3:T(8,128)(2,1)}), bf16[1,2,2,32,8,512]{5,4,1,2,0,3:T(8,128)(2,1)S(1)}, u32[]{:S(2)}, u32[]{:S(2)}) %all-to-all-start.5) | async-done | bytes 1048608 | tf_op jit(solution)/shard_map/all_to_all | solution.py:67
  417.2 2.5 fusion.27
  419.7 1.3 fusion.40
  421.0 1.8 copy.70
  422.8 1.5 reshape.189
  424.4 9.1 %all-to-all-start.6 = ((bf16[64,2,2048]{2,1,0:T(2,128)(2,1)}), bf16[64,2,2048]{2,1,0:T(2,128)(2,1)}, u32[]{:S(2)}, u32[]{:S(2)}) async-start(bf16[64,2,2048]{2,1,0:T(2,128)(2,1)} %reshape.189), calls=%async_computation.6 | async-start | bytes 1048576 | tf_op jit(solution)/shard_map/all_to_all | solution.py:95
  433.5 1.3 copy.74
  434.8 62.7 %all-to-all-done.6 = bf16[64,2,2048]{2,1,0:T(2,128)(2,1)} async-done(((bf16[64,2,2048]{2,1,0:T(2,128)(2,1)}), bf16[64,2,2048]{2,1,0:T(2,128)(2,1)}, u32[]{:S(2)}, u32[]{:S(2)}) %all-to-all-start.6) | async-done | bytes 524320 | tf_op jit(solution)/shard_map/all_to_all | solution.py:95
  497.5 2.3 reshape.190
  499.9 1.6 copy.72
  501.6 2.2 copy.73
  (47 shorter events, 7.8 us)
Async XLA Ops:
  0.6 419.1 %copy-start = (bf16[128,64]{0,1:T(8,128)(2,1)S(1)}, bf16[128,64]{0,1:T(8,128)(2,1)}, u32[]{:S(2)}) copy-start(bf16[128,64]{0,1:T(8,128)(2,1)} %param.20) | copy-start | bytes 49156
  0.7 2.1 copy-start.3
  0.7 24.1 %copy-start.8 = (f32[2,128]{1,0:T(2,128)S(1)}, f32[2,128]{1,0:T(2,128)}, u32[]{:S(2)}) copy-start(f32[2,128]{1,0:T(2,128)} %param.15) | copy-start | bytes 3076
  0.7 24.1 %copy-start.9 = (f32[2,128]{1,0:T(2,128)S(1)}, f32[2,128]{1,0:T(2,128)}, u32[]{:S(2)}) copy-start(f32[2,128]{1,0:T(2,128)} %param.14) | copy-start | bytes 3076
  0.7 24.1 %copy-start.6 = (f32[5,128]{1,0:T(8,128)S(1)}, f32[5,128]{1,0:T(8,128)}, u32[]{:S(2)}) copy-start(f32[5,128]{1,0:T(8,128)} %param.17) | copy-start | bytes 7684
  26.7 6.4 %copy-start.1 = (f32[5,128,8,512]{3,1,0,2:T(8,128)}, f32[5,128,8,512]{3,1,0,2:T(8,128)S(1)}, u32[]{:S(2)}) copy-start(f32[5,128,8,512]{3,1,0,2:T(8,128)S(1)} %add_bitcast_fusion) | copy-start | bytes 31457284
  35.6 3.5 copy-start.7
  59.1 5.9 %all-to-all-start.2 = ((bf16[32,2,2,1,8,512]{5,4,2,0,3,1:T(8,128)(2,1)}), bf16[32,2,2,1,8,512]{5,4,2,0,3,1:T(8,128)(2,1)S(1)}, u32[]{:S(2)}, u32[]{:S(2)}) async-start(bf16[32,2,2,1,8,512]{5,4,2,0,3,1:T(8,128)(2,1)} %get-tuple-element.16), calls=%async_computation.2 | async-start | bytes 2097152 | tf_op jit(solution)/shard_map/all_to_all | solution.py:54
  65.0 118.1 %all-to-all-start.1 = ((bf16[32,1,2,1,16,512]{5,4,2,3,1,0:T(8,128)(2,1)}), bf16[32,1,2,1,16,512]{5,4,2,3,1,0:T(8,128)(2,1)S(1)}, u32[]{:S(2)}, u32[]{:S(2)}) async-start(bf16[32,1,2,1,16,512]{5,4,2,3,1,0:T(8,128)(2,1)} %bitcast.137), calls=%async_computation.1 | async-start | bytes 2097152 | tf_op jit(solution)/shard_map/all_to_all | solution.py:46
  183.0 112.5 %all-to-all-start.3 = ((bf16[32,1,2,1,16,512]{5,4,2,3,1,0:T(8,128)(2,1)}), bf16[32,1,2,1,16,512]{5,4,2,3,1,0:T(8,128)(2,1)S(1)}, u32[]{:S(2)}, u32[]{:S(2)}) async-start(bf16[32,1,2,1,16,512]{5,4,2,3,1,0:T(8,128)(2,1)} %bitcast.138), calls=%async_computation.3 | async-start | bytes 2097152 | tf_op jit(solution)/shard_map/all_to_all | solution.py:53
  192.1 103.5 %copy-start.2 = (bf16[1,1,2,32,1,16,512]{6,5,3,2,4,1,0:T(8,128)(2,1)S(1)}, bf16[1,1,2,32,1,16,512]{6,5,3,2,4,1,0:T(8,128)(2,1)}, u32[]{:S(2)}) copy-start(bf16[1,1,2,32,1,16,512]{6,5,3,2,4,1,0:T(8,128)(2,1)} %copy.57) | copy-start | bytes 3145732
  302.6 8.9 %copy-start.5 = (bf16[64,128]{1,0:T(8,128)(2,1)S(1)}, bf16[64,128]{1,0:T(8,128)(2,1)}, u32[]{:S(2)}) copy-start(bf16[64,128]{1,0:T(8,128)(2,1)} %param.18) | copy-start | bytes 49156
  303.7 112.5 %all-to-all-start.5 = ((bf16[1,2,2,32,8,512]{5,4,1,2,0,3:T(8,128)(2,1)}), bf16[1,2,2,32,8,512]{5,4,1,2,0,3:T(8,128)(2,1)S(1)}, u32[]{:S(2)}, u32[]{:S(2)}) async-start(bf16[1,2,2,32,8,512]{5,4,1,2,0,3:T(8,128)(2,1)} %copy.65), calls=%async_computation.5 | async-start | bytes 2097152 | tf_op jit(solution)/shard_map/all_to_all | solution.py:67
  313.7 103.4 %copy-start.11 = (f32[128]{0:T(128)S(1)}, f32[128]{0:T(128)}, u32[]{:S(2)}) copy-start(f32[128]{0:T(128)} %param.19) | copy-start | bytes 1540
  417.2 2.6 copy-start.10
  424.4 73.1 %all-to-all-start.6 = ((bf16[64,2,2048]{2,1,0:T(2,128)(2,1)}), bf16[64,2,2048]{2,1,0:T(2,128)(2,1)}, u32[]{:S(2)}, u32[]{:S(2)}) async-start(bf16[64,2,2048]{2,1,0:T(2,128)(2,1)} %reshape.189), calls=%async_computation.6 | async-start | bytes 1048576 | tf_op jit(solution)/shard_map/all_to_all | solution.py:95
  501.6 2.5 copy-start.4
where the time goes:
time: 506 us; the launch traced here: 505 us
  waiting for transfers between devices  373 us (74%)
  starting transfers between devices  42.5 us (8%)
  blocking collectives  33.9 us (7%)
  local copies, waits for them, and re-layouts  32.8 us (6%)
  other arithmetic  15.8 us (3%)
  matrix products  6.45 us (1%)
    all_to_all x1, waiting for transfers between devices, local(): lax.all_to_all(lax.all_to_all(left_blocks, 'col', split_axis=1, concat_ax...  104 us
    all_to_all x1, waiting for transfers between devices, local(): lax.all_to_all(lax.all_to_all(right_blocks, 'col', split_axis=1, concat_a...  103 us
    all_to_all x1, waiting for transfers between devices, local(): lax.all_to_all(lax.all_to_all(product, 'col', split_axis=4, concat_axis=1...  102 us
    all_to_all x1, waiting for transfers between devices, local(): lax.all_to_all(logits.astype(jnp.bfloat16), ('row', 'col'), split_axis=1,...  62.7 us
    all_gather x1, blocking collectives, local(): lax.all_gather(w_in, 'col', axis=2, tiled=True)  22 us
    all_to_all x1, starting transfers between devices, local(): lax.all_to_all(lax.all_to_all(left_blocks, 'col', split_axis=1, concat_ax...  13.4 us
  transfers between devices with their start and end apart: 5, of which 5 were waited for; matrix products, arithmetic and copies ran while one was open for 1% of the time, Pallas kernels for 0%

commit v1 on v0

v1 whole, which is shorter than its diff:
```python
import functools

import jax
import jax.numpy as jnp
from jax import lax
from jax.experimental import pallas as pl
from jax.experimental.pallas import tpu as pltpu
from jax.sharding import PartitionSpec as P

F32 = jnp.float32
BF16 = jnp.bfloat16
NT = (((1,), (1,)), ((), ()))
TN = (((0,), (0,)), ((), ()))


def dot(a, b, dims):
    return lax.dot_general(a, b, dims, preferred_element_type=F32)


def input_norm(pair_ref, gain_ref, shift_ref):
    x = pair_ref[...].astype(F32)
    x = x.reshape(-1, x.shape[-1])
    centred = x - jnp.mean(x, axis=-1, keepdims=True)
    spread = jnp.mean(centred * centred, axis=-1, keepdims=True)
    normed = centred * lax.rsqrt(spread + 0.1) * gain_ref[0:1] + shift_ref[0:1]
    return normed.astype(BF16)


def sides_kernel(mask_sref, pair_ref, maskk_ref, w_ref, b_ref, gain_ref, shift_ref, out_ref, stage):
    rows, width, chans = pair_ref.shape
    share = out_ref.shape[1] // 2
    chips = out_ref.shape[0]
    base = (lax.axis_index("row") * lax.axis_size("col") + lax.axis_index("col")) * rows
    normed = input_norm(pair_ref, gain_ref, shift_ref)
    bias = jnp.transpose(jnp.concatenate([b_ref[...], jnp.zeros((3, chans), F32)], axis=0))
    mask_k = maskk_ref[...].astype(F32)
    for side in range(2):
        value = dot(w_ref[2 * side], normed, NT) + bias[:, 2 * side : 2 * side + 1]
        gate = dot(w_ref[2 * side + 1], normed, NT) + bias[:, 2 * side + 1 : 2 * side + 2]
        value = jax.nn.sigmoid(gate) * value
        for r in range(rows):
            mask = mask_k * mask_sref[base + r].astype(F32)
            part = value[:, r * width : (r + 1) * width] * mask
            for c in range(share):
                stage[pl.ds((side * share + c) * rows + r, chips, stride=2 * share * rows), :] = part[
                    c * chips : (c + 1) * chips
                ]
    out_ref[...] = stage[...].reshape(out_ref.shape).astype(BF16)


def make_sides(pair, mask, w_t, b_in, gain, shift, chips):
    rows, length, chans = pair.shape
    share = chans // chips
    width = 128
    whole = lambda *shape: pl.BlockSpec(shape, lambda k: (0,) * len(shape))
    return pl.pallas_call(
        sides_kernel,
        grid=(length // width,),
        in_specs=[
            pl.BlockSpec(memory_space=pltpu.SMEM),
            pl.BlockSpec((rows, width, chans), lambda k: (0, k, 0)),
            pl.BlockSpec((1, width), lambda k: (0, k)),
            whole(*w_t.shape),
            whole(*b_in.shape),
            whole(*gain.shape),
            whole(*shift.shape),
        ],
        out_specs=pl.BlockSpec((chips, 2 * share, rows, width), lambda k: (0, 0, 0, k)),
        out_shape=jax.ShapeDtypeStruct((chips, 2 * share, rows, length), BF16),
        scratch_shapes=[pltpu.VMEM((chips * 2 * share * rows, width), F32)],
        name="sides",
    )(mask, pair, mask.reshape(1, length), w_t, b_in, gain, shift)


def gate_kernel(pair_ref, w_ref, b_ref, gain_ref, shift_ref, out_ref):
    normed = input_norm(pair_ref, gain_ref, shift_ref)
    pre = dot(normed, w_ref[4], NT) + b_ref[4:5]
    out_ref[...] = jax.nn.sigmoid(pre).reshape(out_ref.shape)


def make_gate(pair, w_t, b_in, gain, shift):
    rows, length, chans = pair.shape
    whole = lambda *shape: pl.BlockSpec(shape, lambda r: (0,) * len(shape))
    return pl.pallas_call(
        gate_kernel,
        grid=(rows // 2,),
        in_specs=[
            pl.BlockSpec((2, length, chans), lambda r: (r, 0, 0)),
            whole(*w_t.shape),
            whole(*b_in.shape),
            whole(*gain.shape),
            whole(*shift.shape),
        ],
        out_specs=pl.BlockSpec((2, length, chans), lambda r: (r, 0, 0)),
        out_shape=jax.ShapeDtypeStruct((rows, length, chans), F32),
        cost_estimate=pl.CostEstimate(
            flops=2 * rows * length * chans * chans, bytes_accessed=rows * length * chans * 6, transcendentals=0
        ),
        name="gate",
    )(pair, w_t, b_in, gain, shift)


def triangle_kernel(left_ref, right_ref, other_ref, out_ref):
    chips, _, rows, length = left_ref.shape
    half = chips * rows
    left = left_ref[...].reshape(half, length)
    own = dot(left, right_ref[...].reshape(half, length), NT).astype(BF16)
    other = dot(left, other_ref[...].reshape(half, length), NT).astype(BF16)
    core = lax.axis_index("col")

    def put(first, second):
        out_ref[:, :, :, 0:half] = first.reshape(chips, 1, rows, half)
        out_ref[:, :, :, half : 2 * half] = second.reshape(chips, 1, rows, half)

    pl.when(core == 0)(lambda: put(own, other))
    pl.when(core != 0)(lambda: put(other, own))


def make_triangle(sides, other):
    chips, double, rows, length = sides.shape
    share = double // 2
    block = (chips, 1, rows, length)
    return pl.pallas_call(
        triangle_kernel,
        grid=(share,),
        in_specs=[
            pl.BlockSpec(block, lambda c: (0, c, 0, 0)),
            pl.BlockSpec(block, lambda c: (0, share + c, 0, 0)),
            pl.BlockSpec(block, lambda c: (0, c, 0, 0)),
        ],
        out_specs=pl.BlockSpec(block, lambda c: (0, c, 0, 0)),
        out_shape=jax.ShapeDtypeStruct((chips, share, rows, 2 * chips * rows), BF16),
        name="triangle",
    )(sides, sides, other)


def finish_kernel(
    prod_ref,
    gate_ref,
    pair_ref,
    w_ref,
    b_ref,
    cols_ref,
    headw_ref,
    headb_ref,
    headbt_ref,
    update_ref,
    send_ref,
    own_ref,
    stage,
    sendst,
):
    chans, rows, width = prod_ref.shape
    bins = headw_ref.shape[1]
    core = pl.program_id(1)
    x = prod_ref[...].astype(F32)
    centred = x - jnp.mean(x, axis=0, keepdims=True)
    spread = jnp.mean(centred * centred, axis=0, keepdims=True)
    stage[...] = (centred * lax.rsqrt(spread + 1.0)).reshape(chans * rows, width)
    gain, shift = cols_ref[:, 0:1], cols_ref[:, 1:2]
    b_out = b_ref[...]
    head_w = headw_ref[...]
    head_two = jnp.concatenate([head_w, head_w], axis=1)
    lane = lax.broadcasted_iota(jnp.int32, (width, 2 * bins), 1)
    mine = (lane >= bins) == (core == 1)
    for r in range(rows):
        normed = (stage[pl.ds(r, chans, stride=rows), :] * gain + shift).astype(BF16)
        mixed = dot(normed, w_ref[...], TN) + b_out
        gate = gate_ref[r].reshape(width, chans)
        update = (gate * mixed).astype(BF16)
        update_ref[r] = update.reshape(update_ref.shape[1:])
        pair = pair_ref[r].reshape(width, chans)
        new_pair = (pair.astype(F32) + update.astype(F32)).astype(BF16)
        own_ref[pl.ds(r, bins, stride=rows), :] = dot(head_w, new_pair, (((0,), (1,)), ((), ()))) + headbt_ref[...]
        logits = dot(new_pair, head_two, (((1,), (0,)), ((), ()))) + headb_ref[...]
        at = pl.ds(r, width, stride=rows)

        @pl.when(core == 0)
        def _():
            sendst[at, :] = logits

        @pl.when(core == 1)
        def _():
            sendst[at, :] = jnp.where(mine, logits, sendst[at, :])

    @pl.when(core == 1)
    def _():
        send_ref[...] = sendst[...].reshape(send_ref.shape).astype(BF16)


def make_finish(prod, gate, pair, w_out, b_out, cols, head_w, head_b):
    chips = prod.shape[0]
    rows, length, chans = pair.shape
    bins = head_w.shape[1]
    cores = 2
    width = 128
    steps = length // (cores * width)
    near = chips // steps
    prod = prod.reshape(chans, rows, length)
    view = (rows, chips, cores, rows, chans)
    block = (rows, near, 1, rows, chans)
    at = lambda z, t: (0, z, t, 0, 0)
    whole = lambda *shape: pl.BlockSpec(shape, lambda z, t: (0,) * len(shape))
    head_row = jnp.concatenate([head_b, head_b]).reshape(1, 2 * bins)
    update, send, own = pl.pallas_call(
        finish_kernel,
        grid=(steps, cores),
        in_specs=[
            pl.BlockSpec((chans, rows, width), lambda z, t: (0, 0, t * steps + z)),
            pl.BlockSpec(block, at),
            pl.BlockSpec(block, at),
            whole(*w_out.shape),
            whole(1, chans),
            whole(*cols.shape),
            whole(*head_w.shape),
            whole(1, 2 * bins),
            whole(bins, 1),
        ],
        out_specs=[
            pl.BlockSpec(block, at),
            pl.BlockSpec((near, rows, rows, 2 * bins), lambda z, t: (z, 0, 0, 0)),
            pl.BlockSpec((bins * rows, width), lambda z, t: (0, t * steps + z)),
        ],
        out_shape=[
            jax.ShapeDtypeStruct(view, BF16),
            jax.ShapeDtypeStruct((chips, rows, rows, 2 * bins), BF16),
            jax.ShapeDtypeStruct((bins * rows, length), F32),
        ],
        scratch_shapes=[
            pltpu.VMEM((chans * rows, width), F32),
            pltpu.VMEM((near * rows * rows, 2 * bins), F32),
        ],
        name="finish",
    )(
        prod,
        gate.reshape(view),
        pair.reshape(view),
        w_out,
        b_out.reshape(1, chans),
        cols,
        head_w,
        head_row,
        head_b.reshape(bins, 1),
    )
    return update.reshape(rows, length, chans), send, own


def loss_kernel(mask_sref, own_ref, mine_ref, other_ref, targets_ref, maskk_ref, out_ref, stage):
    chips, rows, _, lanes = mine_ref.shape
    bins = lanes // 2
    half = chips * rows
    length = 2 * half
    core = lax.axis_index("col")
    base = (lax.axis_index("row") * lax.axis_size("col") + core) * rows
    pick_row = lax.broadcasted_iota(jnp.int32, (bins, lanes), 0) + core * bins
    pick = jnp.where(pick_row == lax.broadcasted_iota(jnp.int32, (bins, lanes), 1), 1.0, 0.0).astype(BF16)
    for r in range(rows):
        at = pl.ds(r, bins, stride=rows)
        mine = dot(pick, mine_ref[:, r].reshape(half, lanes), NT)
        other = dot(pick, other_ref[:, r].reshape(half, lanes), NT)
        first = jnp.where(core == 0, mine, other)
        second = jnp.where(core == 0, other, mine)
        for q in range(half // 128):
            stage[q, at, :] = first[:, q * 128 : (q + 1) * 128]
            stage[half // 128 + q, at, :] = second[:, q * 128 : (q + 1) * 128]
    mirrored = jnp.concatenate([stage[q] for q in range(length // 128)], axis=1)
    symmetric = (own_ref[...] + mirrored).reshape(bins, rows, length)
    top = jnp.max(symmetric, axis=0)
    total = jnp.sum(jnp.exp(symmetric - top[None]), axis=0)
    bin_index = lax.broadcasted_iota(jnp.int32, (bins, rows, length), 0)
    picked = jnp.sum(jnp.where(targets_ref[...][None] == bin_index, symmetric, 0.0), axis=0)
    loss = top + jnp.log(total) - picked
    high = loss.astype(BF16)
    rest = loss - high.astype(F32)
    middle = rest.astype(BF16)
    low = (rest - middle.astype(F32)).astype(BF16)
    spot = lax.broadcasted_iota(jnp.int32, (length, length), 0)
    place = lax.broadcasted_iota(jnp.int32, (length, length), 1)
    come = (place // rows % 2) * half + (place // (2 * rows)) * rows + place % rows
    order = jnp.where(spot == come, 1.0, 0.0).astype(BF16)
    natural = dot(high, order, (((1,), (0,)), ((), ())))
    natural += dot(middle, order, (((1,), (0,)), ((), ())))
    natural += dot(low, order, (((1,), (0,)), ((), ())))
    row = lax.broadcasted_iota(jnp.int32, (rows, length), 0)
    mask_i = jnp.zeros((rows, length), F32)
    for r in range(rows):
        mask_i = jnp.where(row == r, mask_sref[base + r].astype(F32), mask_i)
    out_ref[...] = mask_i * maskk_ref[...].astype(F32) * natural


def make_loss(mask, own, mine, other, targets):
    rows, length = targets.shape
    whole = lambda *shape: pl.BlockSpec(shape, lambda: (0,) * len(shape))
    return pl.pallas_call(
        loss_kernel,
        in_specs=[
            pl.BlockSpec(memory_space=pltpu.SMEM),
            whole(*own.shape),
            whole(*mine.shape),
            whole(*other.shape),
            whole(*targets.shape),
            whole(1, length),
        ],
        out_specs=whole(rows, length),
        out_shape=jax.ShapeDtypeStruct((rows, length), F32),
        scratch_shapes=[pltpu.VMEM((length // 128, own.shape[0], 128), F32)],
        name="loss",
    )(mask, own, mine, other, targets, mask.reshape(1, length))


def local(
    pair, residue_mask, targets, ln_gain, ln_shift, w_in, b_in, w_out, b_out, head_weight, head_bias
):
    rows, length, chans = pair.shape
    chips = lax.axis_size("row")
    share = chans // chips
    swap = functools.partial(lax.ppermute, axis_name="col", perm=[(0, 1), (1, 0)])
    exchange = lambda v: lax.all_to_all(v, "row", split_axis=0, concat_axis=0, tiled=True)
    w_t = lax.all_gather(jnp.transpose(w_in, (0, 2, 1)), "col", axis=1, tiled=True)
    sides = make_sides(pair, residue_mask, w_t, b_in, ln_gain, ln_shift, chips)
    sides = exchange(sides)
    gate = make_gate(pair, w_t, b_in, ln_gain, ln_shift)
    by_owner = lambda v: jnp.swapaxes(v.reshape(share, chips, -1), 0, 1).reshape(chans, -1)
    w_full = by_owner(lax.all_gather(w_out, "col", axis=0, tiled=True))
    cols = by_owner(jnp.stack([ln_gain[1], ln_shift[1]], axis=1))
    targets = jnp.swapaxes(targets.reshape(rows, chips, 2, rows), 1, 2).reshape(rows, length)
    product = make_triangle(sides, swap(sides[:, share:]))
    product = exchange(product)
    update, send, own = make_finish(product, gate, pair, w_full, b_out, cols, head_weight, head_bias)
    mine = exchange(send)
    loss = make_loss(residue_mask, own, mine, swap(mine), targets)
    return (update, loss)


def solution(mesh):
    placed = (
        P(("ga", "row", "col"), None, None),
        P("ga"),
        P(("ga", "row", "col"), None),
        P(),
        P(),
        P(None, None, "col"),
        P(),
        P("col", None),
        P(),
        P(),
        P(),
    )
    return jax.shard_map(
        local,
        mesh=mesh,
        in_specs=placed,
        out_specs=(P(("ga", "row", "col"), None, None), P(("ga", "row", "col"), None)),
        check_vma=False,
    )
```

time: 506 us -> 457 us (0.903)
  waiting for transfers between devices: 373 us -> 97 us
  blocking collectives: 33.9 us -> 306 us
  Pallas kernels: 0 us -> 35.3 us
  starting transfers between devices: 42.5 us -> 10.1 us
  local copies, waits for them, and re-layouts: 32.8 us -> 7.02 us
  other arithmetic: 15.8 us -> 0.59 us
  matrix products: 6.45 us -> 0 us
    all_to_all x5 -> x1, waiting for transfers between devices: 373 us -> 94.4 us  [local(): lax.all_to_all(v, 'row', split_axis=0, concat_axis=0, tiled=True)]
    all_to_all x2, blocking collectives: 9.64 us -> 280 us  [local(): lax.all_to_all(v, 'row', split_axis=0, concat_axis=0, tiled=True)]
    pallas_call x0 -> x5, Pallas kernels: none -> 35.3 us  [the longest x1 15.1 us: make_finish(): pl.pallas_call(finish_kernel, grid=(steps, cores), in_specs=[pl.BlockSpec...]
    all_to_all x5 -> x1, starting transfers between devices: 42.5 us -> 7.95 us  [local(): lax.all_to_all(v, 'row', split_axis=0, concat_axis=0, tiled=True)]
    convert_element_type x3 -> x0, other arithmetic: 8.69 us -> none  [the longest x1 8.28 us: local(): right_side = stacked[1].astype(jnp.bfloat16)]
    div x2 -> x0, local copies, waits for them, and re-layouts: 6.92 us -> none  [local(): left_side = pair_mask * jax.nn.sigmoid(projected[1]) * projected[0]]
    dot_general x4 -> x0, matrix products: 6.45 us -> none  [the longest x1 2.53 us: local(): jnp.einsum('cij,cd->dij', normed_outer, lax.all_gather(w_out, 'col', axis...]
    squeeze x2 -> x0, local copies, waits for them, and re-layouts: 6 us -> none  [the longest x1 3.51 us: local(): left_side = pair_mask * jax.nn.sigmoid(projected[1]) * projected[0]]
  transfers between devices with their start and end apart: 5 -> 3, of which waited for: 5 -> 3; matrix products, arithmetic and copies ran while one was open for 1% -> 1% of each run, Pallas kernels for 0% -> 1%
where the time goes in v1:
time: 457 us
  blocking collectives  306 us (67%)
  waiting for transfers between devices  97 us (21%)
  Pallas kernels  35.3 us (8%)
  starting transfers between devices  10.1 us (2%)
  local copies, waits for them, and re-layouts  7.02 us (2%)
    all_to_all x2, blocking collectives, local(): lax.all_to_all(v, 'row', split_axis=0, concat_axis=0, tiled=True)  280 us
    all_to_all x1, waiting for transfers between devices, local(): lax.all_to_all(v, 'row', split_axis=0, concat_axis=0, tiled=True)  94.4 us
    all_gather x1, blocking collectives, local(): lax.all_gather(jnp.transpose(w_in, (0, 2, 1)), 'col', axis=1, tiled=True)  23.8 us
    pallas_call x1, Pallas kernels, make_finish(): pl.pallas_call(finish_kernel, grid=(steps, cores), in_specs=[pl.BlockSpec...  15.1 us
  transfers between devices with their start and end apart: 3, of which 3 were waited for; matrix products, arithmetic and copies ran while one was open for 1% of the time, Pallas kernels for 1%

profile of v1, /device:TPU:37, one launch (start us, length us, event | category | flops | bytes accessed | tf_op | source)
XLA Modules:
  0.0 456.5 jit_solution(2820363941530703181)
XLA Ops:
  0.6 23.8 %all_gather.6.w_ref = bf16[5,128,128]{2,1,0:T(8,128)(2,1)} all-gather(bf16[5,64,128]{2,1,0:T(8,128)(2,1)} %bitcast.27), channel_id=1, replica_groups=mesh['ga'=4,'row'=32,'col'=2] {'col'}, dimensions={1}, use_global_device_ids=true | all-gather | bytes 245760 | tf_op jit(solution)/shard_map/all_gather | solution.py:319
  24.4 7.9 %sides.1 = bf16[32,8,8,512]{3,2,1,0:T(8,128)(2,1)} custom-call(s32[512]{0:T(512)} %mask_sref.3, bf16[8,512,128]{2,1,0:T(8,128)(2,1)} %pair_ref.3, s32[1,512]{1,0:T(1,128)} %bitcast.28, bf16[5,128,128]{2,1,0:T(8,128)(2,1)} %all_gather.6.w_ref, f32[5,128]{1,0:T(8,128)} %b_ref.3, f32[2,128]{1,0:T(2,128)} %gain_ref.3, f32[2,128]{1,0:T(2,128)} %shift_ref.3), custom_call_target="tpu_custom_call" | custom-call | tf_op jit(solution)/shard_map/sides/pallas_call | solution.py:56
  32.2 208.0 %all_to_all.15.left_ref.right_ref = bf16[32,8,8,512]{3,2,1,0:T(8,128)(2,1)S(1)} all-to-all(bf16[32,8,8,512]{3,2,1,0:T(8,128)(2,1)} %sides.1), channel_id=1, replica_groups=mesh['ga'=4,'row'=32,'col'=2] {'row'}, dimensions={0} | all-to-all | bytes 4194304 | tf_op jit(solution)/shard_map/all_to_all | solution.py:318
  240.3 0.1 slice.12
  240.4 0.7 collective-permute-start
  241.1 2.3 collective-permute-done.other_ref
  243.4 0.0 copy-done
  243.4 1.0 copy-done.3
  244.4 4.5 triangle.1
  248.9 0.0 copy-start.6
  248.9 0.0 copy-start.10
  248.9 8.0 %all-to-all-start.1 = ((bf16[32,4,8,512]{3,2,1,0:T(8,128)(2,1)}), bf16[32,4,8,512]{3,2,1,0:T(8,128)(2,1)S(1)}, u32[]{:S(2)}, u32[]{:S(2)}) async-start(bf16[32,4,8,512]{3,2,1,0:T(8,128)(2,1)} %triangle.1), calls=%async_computation.1 | async-start | bytes 2097152 | tf_op jit(solution)/shard_map/all_to_all | solution.py:318
  256.8 0.0 copy-done.8
  256.9 0.1 stack.7
  257.0 0.1 stack.8
  257.1 0.7 copy.19
  257.8 2.2 all_gather.7
  259.9 0.6 copy.18
  260.6 0.7 copy.20.headw_ref
  261.3 0.7 copy.21.headbt_ref
  262.0 4.6 gate.1
  266.5 0.6 maximum_bitcast_fusion.1.headb_ref
  267.1 94.4 %all-to-all-done.1 = bf16[32,4,8,512]{3,2,1,0:T(8,128)(2,1)S(1)} async-done(((bf16[32,4,8,512]{3,2,1,0:T(8,128)(2,1)}), bf16[32,4,8,512]{3,2,1,0:T(8,128)(2,1)S(1)}, u32[]{:S(2)}, u32[]{:S(2)}) %all-to-all-start.1) | async-done | bytes 1048608 | tf_op jit(solution)/shard_map/all_to_all | solution.py:318
  361.5 1.0 copy-done.1
  362.5 15.1 %finish.1 = (bf16[8,32,2,8,128]{4,3,2,1,0:T(8,128)(2,1)}, bf16[32,8,8,128]{3,2,1,0:T(8,128)(2,1)}, f32[512,512]{1,0:T(8,128)}) custom-call(bf16[128,8,512]{2,1,0:T(8,128)(2,1)} %bitcast.22, f32[8,32,2,8,128]{4,3,2,1,0:T(8,128)} %bitcast.21, bf16[8,32,2,8,128]{4,3,2,1,0:T(8,128)(2,1)} %bitcast.20, bf16[128,128]{1,0:T(8,128)(2,1)} %bitcast.25, ...), custom_call_target="tpu_custom_call" | custom-call | tf_op jit(solution)/shard_map/finish/pallas_call | solution.py:205
  377.5 71.9 %all_to_all.16.mine_ref = bf16[32,8,8,128]{3,2,1,0:T(8,128)(2,1)S(1)} all-to-all(bf16[32,8,8,128]{3,2,1,0:T(8,128)(2,1)} %get-tuple-element.7), channel_id=1, replica_groups=mesh['ga'=4,'row'=32,'col'=2] {'row'}, dimensions={0} | all-to-all | bytes 1048576 | tf_op jit(solution)/shard_map/all_to_all | solution.py:318
  449.5 1.4 collective-permute-start.1
  450.8 0.4 reshape.60
  451.3 0.8 reshape.61.targets_ref
  452.1 0.3 collective-permute-done.1.other_ref
  452.4 0.8 copy-done.4
  453.2 3.4 loss.1
  (18 shorter events, 0.1 us)
Async XLA Ops:
  240.3 3.1 copy-start
  240.4 3.0 collective-permute-start
  243.4 1.0 copy-start.3
  248.8 8.0 %copy-start.8 = (f32[2,128]{1,0:T(2,128)S(1)}, f32[2,128]{1,0:T(2,128)}, u32[]{:S(2)}) copy-start(f32[2,128]{1,0:T(2,128)} %gain_ref.3) | copy-start | bytes 3076
  248.8 8.0 %copy-start.9 = (f32[2,128]{1,0:T(2,128)S(1)}, f32[2,128]{1,0:T(2,128)}, u32[]{:S(2)}) copy-start(f32[2,128]{1,0:T(2,128)} %shift_ref.3) | copy-start | bytes 3076
  248.9 8.9 %copy-start.5 = (bf16[64,128]{1,0:T(8,128)(2,1)S(1)}, bf16[64,128]{1,0:T(8,128)(2,1)}, u32[]{:S(2)}) copy-start(bf16[64,128]{1,0:T(8,128)(2,1)} %param.18) | copy-start | bytes 49156
  248.9 11.7 %copy-start.6 = (bf16[128,64]{0,1:T(8,128)(2,1)S(1)}, bf16[128,64]{0,1:T(8,128)(2,1)}, u32[]{:S(2)}) copy-start(bf16[128,64]{0,1:T(8,128)(2,1)} %param.20) | copy-start | bytes 49156
  248.9 12.4 %copy-start.10 = (f32[64]{0:T(128)S(1)}, f32[64]{0:T(128)}, u32[]{:S(2)}) copy-start(f32[64]{0:T(128)} %param.21) | copy-start | bytes 772
  248.9 112.6 %all-to-all-start.1 = ((bf16[32,4,8,512]{3,2,1,0:T(8,128)(2,1)}), bf16[32,4,8,512]{3,2,1,0:T(8,128)(2,1)S(1)}, u32[]{:S(2)}, u32[]{:S(2)}) async-start(bf16[32,4,8,512]{3,2,1,0:T(8,128)(2,1)} %triangle.1), calls=%async_computation.1 | async-start | bytes 2097152 | tf_op jit(solution)/shard_map/all_to_all | solution.py:318
  361.5 1.0 copy-start.1
  362.5 88.4 %copy-start.7 = (s32[8,512]{1,0:T(8,128)S(1)}, s32[8,512]{1,0:T(8,128)}, u32[]{:S(2)}) copy-start(s32[8,512]{1,0:T(8,128)} %param.13) | copy-start | bytes 49156
  449.5 2.9 copy-start.2
  449.5 2.9 collective-permute-start.1
  452.4 0.8 copy-start.4

commit v2 on v1

v2 whole, which is shorter than its diff:
```python
import functools

import jax
import jax.numpy as jnp
from jax import lax
from jax.experimental import pallas as pl
from jax.experimental.pallas import tpu as pltpu
from jax.sharding import PartitionSpec as P

F32 = jnp.float32
BF16 = jnp.bfloat16
NT = (((1,), (1,)), ((), ()))
TN = (((0,), (0,)), ((), ()))


def dot(a, b, dims):
    return lax.dot_general(a, b, dims, preferred_element_type=F32)


def whole(*shape):
    return pl.BlockSpec(shape, lambda *_: (0,) * len(shape))


def in_vmem():
    return pl.BlockSpec(memory_space=pltpu.VMEM)


def pinned(*arrays):
    return [pltpu.with_memory_space_constraint(a, pltpu.VMEM) for a in arrays]


def norm_kernel(pair_ref, gain_ref, shift_ref, out_ref):
    chans = pair_ref.shape[-1]
    pair = pair_ref[...].reshape(-1, chans)
    centred = pair.astype(F32) - dot(pair, jnp.full((chans, chans), 1.0 / chans, BF16), NT)
    spread = jnp.mean(centred * centred, axis=-1, keepdims=True)
    normed = centred * lax.rsqrt(spread + 0.1) * gain_ref[0:1] + shift_ref[0:1]
    rows = pair_ref.shape[0]
    out_ref[pl.ds(pl.program_id(0) * rows, rows)] = normed.astype(BF16).reshape(pair_ref.shape)


def make_norm(pair, gain, shift):
    rows, length, chans = pair.shape
    return pl.pallas_call(
        norm_kernel,
        grid=(rows // 2,),
        in_specs=[
            pl.BlockSpec((2, length, chans), lambda r: (r, 0, 0)),
            whole(*gain.shape),
            whole(*shift.shape),
        ],
        out_specs=in_vmem(),
        out_shape=jax.ShapeDtypeStruct(pair.shape, BF16),
        cost_estimate=pl.CostEstimate(
            flops=rows * length * chans * 100, bytes_accessed=rows * length * chans * 4, transcendentals=0
        ),
        name="norm",
    )(pair, gain, shift)


def weight(mine_ref, other_ref, n):
    mine, other = mine_ref[n], other_ref[n]
    first = lax.axis_index("col") == 0
    return jnp.concatenate([jnp.where(first, mine, other), jnp.where(first, other, mine)], axis=0)


def side_kernel(side, lag, mask_sref, normed_ref, maskk_ref, mine_ref, other_ref, b_ref, out_ref, stage):
    rows, length, chans = normed_ref.shape
    chips, share = out_ref.shape[:2]
    width = stage.shape[1]
    pitch = stage.shape[0] // chips
    core = lax.axis_index("col")
    if lag:
        pl.when(core == 1)(lambda: pl.delay(lag))
    base = (lax.axis_index("row") * lax.axis_size("col") + core) * rows
    bias = jnp.transpose(jnp.concatenate([b_ref[...], jnp.zeros((3, chans), F32)], axis=0))
    w_value = weight(mine_ref, other_ref, 2 * side)
    w_gate = weight(mine_ref, other_ref, 2 * side + 1)
    for k in range(length // width):
        normed = normed_ref[:, k * width : (k + 1) * width, :].reshape(rows * width, chans)
        value = dot(w_value, normed, NT) + bias[:, 2 * side : 2 * side + 1]
        gate = dot(w_gate, normed, NT) + bias[:, 2 * side + 1 : 2 * side + 2]
        value = jax.nn.sigmoid(gate) * value
        mask_k = maskk_ref[:, k * width : (k + 1) * width].astype(F32)
        for r in range(rows):
            part = value[:, r * width : (r + 1) * width] * (mask_k * mask_sref[base + r].astype(F32))
            for c in range(share):
                stage[pl.ds(c * rows + r, chips, stride=pitch), :] = part[c * chips : (c + 1) * chips]
        for z in range(chips):
            block = stage[z * pitch : z * pitch + share * rows, :].reshape(share, rows, width)
            out_ref[z, :, :, k * width : (k + 1) * width] = block.astype(BF16)


def make_side(side, lag, normed, mask, w_mine, w_other, b_in, chips):
    rows, length, chans = normed.shape
    share = chans // chips
    return pl.pallas_call(
        functools.partial(side_kernel, side, lag),
        in_specs=[pl.BlockSpec(memory_space=pltpu.SMEM)] + [in_vmem()] * 5,
        out_specs=in_vmem(),
        out_shape=jax.ShapeDtypeStruct((chips, share, rows, length), BF16),
        scratch_shapes=[pltpu.VMEM((chips * (share * rows + 8), 128), F32)],
        cost_estimate=pl.CostEstimate(
            flops=4 * rows * length * chans * chans, bytes_accessed=rows * length * chans * 4, transcendentals=0
        ),
        name=("left", "right")[side],
    )(mask, normed, mask.reshape(1, length), w_mine, w_other, b_in)


def gate_kernel(normed_ref, mine_ref, other_ref, b_ref, out_ref):
    normed = normed_ref[pl.program_id(0)]
    pre = dot(normed, weight(mine_ref, other_ref, 4), NT) + b_ref[4:5]
    out_ref[0] = jax.nn.sigmoid(pre)


def make_gate(normed, w_mine, w_other, b_in):
    rows, length, chans = normed.shape
    return pl.pallas_call(
        gate_kernel,
        grid=(rows,),
        in_specs=[in_vmem()] * 4,
        out_specs=pl.BlockSpec((1, length, chans), lambda r: (r, 0, 0)),
        out_shape=jax.ShapeDtypeStruct((rows, length, chans), F32),
        cost_estimate=pl.CostEstimate(
            flops=2 * rows * length * chans * chans, bytes_accessed=rows * length * chans * 6, transcendentals=0
        ),
        name="gate",
    )(normed, w_mine, w_other, b_in)


def triangle_kernel(left_ref, right_ref, other_ref, out_ref):
    chips, share, rows, length = left_ref.shape
    half = chips * rows
    core = lax.axis_index("col")
    for c in range(share):
        left = left_ref[:, c].reshape(half, length)
        mine = right_ref[:, c].reshape(half, length)
        other = other_ref[:, c].reshape(half, length)
        first = jnp.where(core == 0, mine, other)
        second = jnp.where(core == 0, other, mine)
        out_ref[:, c, :, 0:half] = dot(left, first, NT).astype(BF16).reshape(chips, rows, half)
        out_ref[:, c, :, half : 2 * half] = dot(left, second, NT).astype(BF16).reshape(chips, rows, half)


def make_triangle(left, right, other):
    return pl.pallas_call(
        triangle_kernel,
        in_specs=[in_vmem()] * 3,
        out_specs=in_vmem(),
        out_shape=jax.ShapeDtypeStruct(left.shape, BF16),
        name="triangle",
    )(*pinned(left), right, *pinned(other))


def finish_kernel(
    prod_ref,
    gate_ref,
    pair_ref,
    w_ref,
    b_ref,
    cols_ref,
    headt_ref,
    headb_ref,
    headbt_ref,
    update_ref,
    send_ref,
    own_ref,
    stage,
    sendst,
):
    chans, rows, _ = prod_ref.shape
    width = stage.shape[2]
    bins = headt_ref.shape[0]
    near = update_ref.shape[1]
    step, steps = pl.program_id(0), pl.num_programs(0)
    gain, shift = cols_ref[:, 0:1], cols_ref[:, 1:2]
    head_t = headt_ref[...]
    head_two = jnp.concatenate([head_t, head_t], axis=0)
    flat = (rows * width, chans)
    logits = []
    for t in range(2):
        at = pl.multiple_of((t * steps + step) * width, width)
        x = prod_ref[:, :, pl.ds(at, width)].astype(F32)
        centred = x - jnp.mean(x, axis=0, keepdims=True)
        spread = jnp.mean(centred * centred, axis=0, keepdims=True)
        stage[t] = (centred * lax.rsqrt(spread + 1.0)).reshape(chans * rows, width)
        normed = [stage[t, pl.ds(r, chans, stride=rows), :] * gain + shift for r in range(rows)]
        normed = jnp.concatenate(normed, axis=1).astype(BF16)
        mixed = dot(normed, w_ref[...], TN) + b_ref[...]
        update = (gate_ref[:, :, t].reshape(flat) * mixed).astype(BF16)
        update_ref[:, :, t] = update.reshape(rows, near, rows, chans)
        pair = pair_ref[:, :, t].reshape(flat)
        new_pair = (pair.astype(F32) + update.astype(F32)).astype(BF16)
        own = dot(head_t, new_pair, NT) + headbt_ref[...]
        for r in range(rows):
            own_ref[t * steps + step, pl.ds(r, bins, stride=rows), :] = own[:, r * width : (r + 1) * width]
        logits.append(dot(new_pair, head_two, NT) + headb_ref[...])
    lane = lax.broadcasted_iota(jnp.int32, logits[0].shape, 1)
    both = jnp.where(lane < bins, logits[0], logits[1])
    for r in range(rows):
        sendst[pl.ds(r, width, stride=rows), :] = both[r * width : (r + 1) * width]
    send_ref[pl.ds(step * near, near)] = sendst[...].reshape(near, rows, rows, 2 * bins).astype(BF16)


def make_finish(prod, gate, pair, w_out, b_out, cols, head_w, head_b):
    chips = prod.shape[0]
    rows, length, chans = pair.shape
    bins = head_w.shape[1]
    cores = 2
    width = 128
    steps = length // (cores * width)
    near = chips // steps
    prod = prod.reshape(chans, rows, length)
    view = (rows, chips, cores, rows, chans)
    wide = pl.BlockSpec((rows, near, cores, rows, chans), lambda z: (0, z, 0, 0, 0))
    head_row = jnp.concatenate([head_b, head_b]).reshape(1, 2 * bins)
    update, send, own = pl.pallas_call(
        finish_kernel,
        grid=(steps,),
        in_specs=[
            in_vmem(),
            wide,
            wide,
            whole(*w_out.shape),
            whole(1, chans),
            whole(*cols.shape),
            whole(bins, chans),
            whole(1, 2 * bins),
            whole(bins, 1),
        ],
        out_specs=[wide, in_vmem(), in_vmem()],
        out_shape=[
            jax.ShapeDtypeStruct(view, BF16),
            jax.ShapeDtypeStruct((chips, rows, rows, 2 * bins), BF16),
            jax.ShapeDtypeStruct((length // width, bins * rows, width), F32),
        ],
        scratch_shapes=[
            pltpu.VMEM((2, chans * rows, width), F32),
            pltpu.VMEM((near * rows * rows, 2 * bins), F32),
        ],
        name="finish",
    )(
        *pinned(prod),
        gate.reshape(view),
        pair.reshape(view),
        w_out,
        b_out.reshape(1, chans),
        cols,
        jnp.transpose(head_w),
        head_row,
        head_b.reshape(bins, 1),
    )
    return update.reshape(rows, length, chans), send, own


def loss_kernel(mask_sref, own_ref, mine_ref, other_ref, targets_ref, maskk_ref, out_ref, stage):
    chips, rows, _, lanes = mine_ref.shape
    bins = lanes // 2
    half = chips * rows
    length = 2 * half
    core = lax.axis_index("col")
    base = (lax.axis_index("row") * lax.axis_size("col") + core) * rows
    pick_row = lax.broadcasted_iota(jnp.int32, (bins, lanes), 0) + core * bins
    pick = jnp.where(pick_row == lax.broadcasted_iota(jnp.int32, (bins, lanes), 1), 1.0, 0.0).astype(BF16)
    for r in range(rows):
        at = pl.ds(r, bins, stride=rows)
        mine = dot(pick, mine_ref[:, r].reshape(half, lanes), NT)
        other = dot(pick, other_ref[:, r].reshape(half, lanes), NT)
        first = jnp.where(core == 0, mine, other)
        second = jnp.where(core == 0, other, mine)
        for q in range(half // 128):
            stage[q, at, :] = first[:, q * 128 : (q + 1) * 128]
            stage[half // 128 + q, at, :] = second[:, q * 128 : (q + 1) * 128]
    symmetric = jnp.concatenate([own_ref[q] + stage[q] for q in range(length // 128)], axis=1)
    symmetric = symmetric.reshape(bins, rows, length)
    top = jnp.max(symmetric, axis=0)
    total = jnp.sum(jnp.exp(symmetric - top[None]), axis=0)
    bin_index = lax.broadcasted_iota(jnp.int32, (bins, rows, length), 0)
    picked = jnp.sum(jnp.where(targets_ref[...][None] == bin_index, symmetric, 0.0), axis=0)
    loss = top + jnp.log(total) - picked
    high = loss.astype(BF16)
    rest = loss - high.astype(F32)
    middle = rest.astype(BF16)
    low = (rest - middle.astype(F32)).astype(BF16)
    spot = lax.broadcasted_iota(jnp.int32, (length, length), 0)
    place = lax.broadcasted_iota(jnp.int32, (length, length), 1)
    come = (place // rows % 2) * half + (place // (2 * rows)) * rows + place % rows
    order = jnp.where(spot == come, 1.0, 0.0).astype(BF16)
    natural = dot(high, order, (((1,), (0,)), ((), ())))
    natural += dot(middle, order, (((1,), (0,)), ((), ())))
    natural += dot(low, order, (((1,), (0,)), ((), ())))
    row = lax.broadcasted_iota(jnp.int32, (rows, length), 0)
    mask_i = jnp.zeros((rows, length), F32)
    for r in range(rows):
        mask_i = jnp.where(row == r, mask_sref[base + r].astype(F32), mask_i)
    out_ref[...] = mask_i * maskk_ref[...].astype(F32) * natural


def make_loss(mask, own, mine, other, targets):
    rows, length = targets.shape
    return pl.pallas_call(
        loss_kernel,
        in_specs=[pl.BlockSpec(memory_space=pltpu.SMEM)] + [in_vmem()] * 5,
        out_specs=in_vmem(),
        out_shape=jax.ShapeDtypeStruct((rows, length), F32),
        scratch_shapes=[pltpu.VMEM(own.shape, F32)],
        name="loss",
    )(mask, own, *pinned(mine, other), targets, mask.reshape(1, length))


LAG_NS = 35000


def local(
    pair, residue_mask, targets, ln_gain, ln_shift, w_in, b_in, w_out, b_out, head_weight, head_bias
):
    rows, length, chans = pair.shape
    chips = lax.axis_size("row")
    share = chans // chips
    swap = functools.partial(lax.ppermute, axis_name="col", perm=[(0, 1), (1, 0)])
    exchange = lambda v: lax.all_to_all(v, "row", split_axis=0, concat_axis=0, tiled=True)
    by_owner = lambda v: jnp.swapaxes(v.reshape(share, chips, -1), 0, 1).reshape(chans, -1)
    w_mine = jnp.transpose(w_in, (0, 2, 1))
    w_other = swap(w_mine)
    out_other = swap(w_out)
    normed = make_norm(pair, ln_gain, ln_shift)
    right = make_side(1, LAG_NS, normed, residue_mask, w_mine, *pinned(w_other), b_in, chips)
    right, out_other = lax.optimization_barrier((right, out_other))
    right = exchange(right)
    left = make_side(0, 0, normed, residue_mask, w_mine, w_other, b_in, chips)
    gate = make_gate(normed, w_mine, w_other, b_in)
    first = lax.axis_index("col") == 0
    w_full = jnp.concatenate([jnp.where(first, w_out, out_other), jnp.where(first, out_other, w_out)], axis=0)
    w_full = by_owner(w_full)
    cols = by_owner(jnp.stack([ln_gain[1], ln_shift[1]], axis=1))
    targets = jnp.swapaxes(targets.reshape(rows, chips, 2, rows), 1, 2).reshape(rows, length)
    left, targets, w_full, cols = lax.optimization_barrier((left, targets, w_full, cols))
    right_other = swap(right)
    left = exchange(left)
    product = exchange(make_triangle(left, right, right_other))
    update, send, own = make_finish(product, gate, pair, w_full, b_out, cols, head_weight, head_bias)
    mine = exchange(send)
    loss = make_loss(residue_mask, own, mine, swap(mine), targets)
    return (update, loss)


def solution(mesh):
    placed = (
        P(("ga", "row", "col"), None, None),
        P("ga"),
        P(("ga", "row", "col"), None),
        P(),
        P(),
        P(None, None, "col"),
        P(),
        P("col", None),
        P(),
        P(),
        P(),
    )
    return jax.shard_map(
        local,
        mesh=mesh,
        in_specs=placed,
        out_specs=(P(("ga", "row", "col"), None, None), P(("ga", "row", "col"), None)),
        check_vma=False,
    )
```

time: 457 us -> 403 us (0.88)
  blocking collectives: 306 us -> 50.7 us
  waiting for transfers between devices: 97 us -> 234 us
  starting transfers between devices: 10.1 us -> 45.5 us
  Pallas kernels: 35.3 us -> 62.7 us
    all_to_all x2 -> x1, blocking collectives: 280 us -> 50.7 us  [local(): lax.all_to_all(v, 'row', split_axis=0, concat_axis=0, tiled=True)]
    all_to_all x1 -> x3, waiting for transfers between devices: 94.4 us -> 232 us  [local(): lax.all_to_all(v, 'row', split_axis=0, concat_axis=0, tiled=True)]
    pallas_call x4 -> x6, Pallas kernels: 32 us -> 59.6 us  [the longest x2 41.9 us: make_side(): pl.pallas_call(functools.partial(side_kernel, side, lag), in_specs=[pl.Bl...]
    all_gather x2 -> x0, blocking collectives: 25.9 us -> none  [the longest x1 23.8 us: local(): lax.all_gather(jnp.transpose(w_in, (0, 2, 1)), 'col', axis=1, tiled=True)]
    ppermute x1 -> x3, starting transfers between devices: 0.74 us -> 20.8 us  [the longest x1 20.5 us: local(): w_other = swap(w_mine)]
    all_to_all x1 -> x3, starting transfers between devices: 7.95 us -> 24.7 us  [local(): lax.all_to_all(v, 'row', split_axis=0, concat_axis=0, tiled=True)]
  transfers between devices with their start and end apart: 3 -> 7, of which waited for: 3 -> 4; matrix products, arithmetic and copies ran while one was open for 1% -> 1% of each run, Pallas kernels for 1% -> 13%
where the time goes in v2:
time: 403 us; the launch traced here: 398 us
  waiting for transfers between devices  234 us (58%)
  Pallas kernels  62.7 us (16%)
  blocking collectives  50.7 us (13%)
  starting transfers between devices  45.5 us (11%)
    all_to_all x3, waiting for transfers between devices, local(): lax.all_to_all(v, 'row', split_axis=0, concat_axis=0, tiled=True)  232 us
    all_to_all x1, blocking collectives, local(): lax.all_to_all(v, 'row', split_axis=0, concat_axis=0, tiled=True)  50.7 us
    pallas_call x2, Pallas kernels, make_side(): pl.pallas_call(functools.partial(side_kernel, side, lag), in_specs=[pl.Bl...  41.9 us
    all_to_all x3, starting transfers between devices, local(): lax.all_to_all(v, 'row', split_axis=0, concat_axis=0, tiled=True)  24.7 us
    ppermute x1, starting transfers between devices, local(): w_other = swap(w_mine)  20.5 us
  transfers between devices with their start and end apart: 7, of which 4 were waited for; matrix products, arithmetic and copies ran while one was open for 1% of the time, Pallas kernels for 13%

profile of v2, /device:TPU:37, one launch (start us, length us, event | category | flops | bytes accessed | tf_op | source)
XLA Modules:
  0.0 398.0 jit_solution(4567754476771151939)
XLA Ops:
  0.6 20.5 %collective-permute-start = (bf16[5,64,128]{2,1,0:T(8,128)(2,1)}, bf16[5,64,128]{2,1,0:T(8,128)(2,1)S(1)}, u32[]{:S(2)}, u32[]{:S(2)}) collective-permute-start(bf16[5,64,128]{2,1,0:T(8,128)(2,1)} %bitcast.25), channel_id=1, source_target_pairs={{0,1},{1,0},{2,3},{3,2},{4,5},{5,4},{6,7},{7,6},{8,9},{9,8},{10,11... | collective-permute-start | bytes 245768 | tf_op jit(solution)/shard_map/ppermute | solution.py:324
  21.2 0.2 collective-permute-start.1
  21.3 4.1 %norm.1.normed_ref = bf16[8,512,128]{2,1,0:T(8,128)(2,1)} custom-call(bf16[8,512,128]{2,1,0:T(8,128)(2,1)} %pair_ref.1, f32[2,128]{1,0:T(2,128)} %gain_ref.1, f32[2,128]{1,0:T(2,128)} %shift_ref.1), custom_call_target="tpu_custom_call" | custom-call | flops 52428800 | bytes 2097152 | tf_op jit(solution)/shard_map/norm/pallas_call | solution.py:44
  25.4 0.0 collective-permute-done.other_ref
  25.4 0.0 copy-start.5
  25.4 0.0 copy-start.2
  25.4 38.4 %right.1 = bf16[32,4,8,512]{3,2,1,0:T(8,128)(2,1)} custom-call(s32[512]{0:T(512)} %mask_sref.5, bf16[8,512,128]{2,1,0:T(8,128)(2,1)} %norm.1.normed_ref, s32[1,512]{1,0:T(1,128)} %bitcast.32, bf16[5,64,128]{2,1,0:T(8,128)(2,1)} %bitcast.26, bf16[5,64,128]{2,1,0:T(8,128)(2,1)S(1)} %collective-permute-done.other_ref, f32[5,128]{1,0:T(8,128)} %b_ref.5), custom_call_target="tpu_custom_call" | custom-call | flops 268435456 | bytes 2097152 | tf_op jit(solution)/shard_map/right/pallas_call | solution.py:97
  63.9 0.0 collective-permute-done.1
  63.9 13.4 %all-to-all-start.1 = ((bf16[32,4,8,512]{3,2,1,0:T(8,128)(2,1)}), bf16[32,4,8,512]{3,2,1,0:T(8,128)(2,1)S(1)}, u32[]{:S(2)}, u32[]{:S(2)}) async-start(bf16[32,4,8,512]{3,2,1,0:T(8,128)(2,1)} %right.1), calls=%async_computation.1 | async-start | bytes 2097152 | tf_op jit(solution)/shard_map/all_to_all | solution.py:321
  77.3 0.1 stack.7
  77.4 0.1 stack.8
  77.5 0.7 copy.19
  78.2 0.4 reshape.51
  78.7 0.8 reshape.52.targets_ref
  79.5 0.6 copy.18
  80.1 3.4 left.1
  83.6 73.3 %all-to-all-done.1.right_ref = bf16[32,4,8,512]{3,2,1,0:T(8,128)(2,1)S(1)} async-done(((bf16[32,4,8,512]{3,2,1,0:T(8,128)(2,1)}), bf16[32,4,8,512]{3,2,1,0:T(8,128)(2,1)S(1)}, u32[]{:S(2)}, u32[]{:S(2)}) %all-to-all-start.1) | async-done | bytes 1048608 | tf_op jit(solution)/shard_map/all_to_all | solution.py:321
  156.9 6.0 %all-to-all-start = ((bf16[32,4,8,512]{3,2,1,0:T(8,128)(2,1)}), bf16[32,4,8,512]{3,2,1,0:T(8,128)(2,1)S(1)}, u32[]{:S(2)}, u32[]{:S(2)}) async-start(bf16[32,4,8,512]{3,2,1,0:T(8,128)(2,1)} %left.1), calls=%async_computation | async-start | bytes 2097152 | tf_op jit(solution)/shard_map/all_to_all | solution.py:321
  162.9 0.1 collective-permute-start.2
  163.0 78.3 %all-to-all-done.left_ref = bf16[32,4,8,512]{3,2,1,0:T(8,128)(2,1)S(1)} async-done(((bf16[32,4,8,512]{3,2,1,0:T(8,128)(2,1)}), bf16[32,4,8,512]{3,2,1,0:T(8,128)(2,1)S(1)}, u32[]{:S(2)}, u32[]{:S(2)}) %all-to-all-start) | async-done | bytes 1048608 | tf_op jit(solution)/shard_map/all_to_all | solution.py:321
  241.3 0.0 collective-permute-done.2.other_ref
  241.3 2.9 triangle.1
  244.2 5.2 %all-to-all-start.2 = ((bf16[32,4,8,512]{3,2,1,0:T(8,128)(2,1)}), bf16[32,4,8,512]{3,2,1,0:T(8,128)(2,1)S(1)}, u32[]{:S(2)}, u32[]{:S(2)}) async-start(bf16[32,4,8,512]{3,2,1,0:T(8,128)(2,1)} %triangle.1), calls=%async_computation.2 | async-start | bytes 2097152 | tf_op jit(solution)/shard_map/all_to_all | solution.py:321
  249.5 0.7 copy.20.headbt_ref
  250.2 0.6 maximum_bitcast_fusion.1.headb_ref
  250.8 5.2 %gate.1 = f32[8,512,128]{2,1,0:T(8,128)} custom-call(bf16[8,512,128]{2,1,0:T(8,128)(2,1)} %norm.1.normed_ref, bf16[5,64,128]{2,1,0:T(8,128)(2,1)} %bitcast.28, bf16[5,64,128]{2,1,0:T(8,128)(2,1)} %copy-done, f32[5,128]{1,0:T(8,128)} %b_ref.5), custom_call_target="tpu_custom_call" | custom-call | flops 134217728 | bytes 3145728 | tf_op jit(solution)/shard_map/gate/pallas_call | solution.py:118
  256.0 80.7 %all-to-all-done.2 = bf16[32,4,8,512]{3,2,1,0:T(8,128)(2,1)S(1)} async-done(((bf16[32,4,8,512]{3,2,1,0:T(8,128)(2,1)}), bf16[32,4,8,512]{3,2,1,0:T(8,128)(2,1)S(1)}, u32[]{:S(2)}, u32[]{:S(2)}) %all-to-all-start.2) | async-done | bytes 1048608 | tf_op jit(solution)/shard_map/all_to_all | solution.py:321
  336.7 5.5 %finish.1 = (bf16[8,32,2,8,128]{4,3,2,1,0:T(8,128)(2,1)}, bf16[32,8,8,128]{3,2,1,0:T(8,128)(2,1)}, f32[4,512,128]{2,1,0:T(8,128)}) custom-call(bf16[128,8,512]{2,1,0:T(8,128)(2,1)S(1)} %bitcast.21, f32[8,32,2,8,128]{4,3,2,1,0:T(8,128)} %bitcast.22, bf16[8,32,2,8,128]{4,3,2,1,0:T(8,128)(2,1)} %bitcast.23, bf16[128,128]{1,0:T(8,128)(2,1)} %bitcast.30, ...), custom_call_target="tpu_custom_call" | custom-call | tf_op jit(solution)/shard_map/finish/pallas_call | solution.py:217
  342.2 50.7 %all_to_all.20.mine_ref = bf16[32,8,8,128]{3,2,1,0:T(8,128)(2,1)S(1)} all-to-all(bf16[32,8,8,128]{3,2,1,0:T(8,128)(2,1)} %get-tuple-element.18), channel_id=1, replica_groups=mesh['ga'=4,'row'=32,'col'=2] {'row'}, dimensions={0} | all-to-all | bytes 1048576 | tf_op jit(solution)/shard_map/all_to_all | solution.py:321
  393.0 0.0 collective-permute-start.3
  393.0 1.9 collective-permute-done.3.other_ref
  394.9 3.1 loss.1
  (17 shorter events, 0.1 us)
Async XLA Ops:
  0.6 24.8 %collective-permute-start = (bf16[5,64,128]{2,1,0:T(8,128)(2,1)}, bf16[5,64,128]{2,1,0:T(8,128)(2,1)S(1)}, u32[]{:S(2)}, u32[]{:S(2)}) collective-permute-start(bf16[5,64,128]{2,1,0:T(8,128)(2,1)} %bitcast.25), channel_id=1, source_target_pairs={{0,1},{1,0},{2,3},{3,2},{4,5},{5,4},{6,7},{7,6},{8,9},{9,8},{10,11... | collective-permute-start | bytes 245768 | tf_op jit(solution)/shard_map/ppermute | solution.py:324
  21.2 42.7 %collective-permute-start.1 = (bf16[64,128]{1,0:T(8,128)(2,1)}, bf16[64,128]{1,0:T(8,128)(2,1)S(1)}, u32[]{:S(2)}, u32[]{:S(2)}) collective-permute-start(bf16[64,128]{1,0:T(8,128)(2,1)} %param.18), channel_id=1, source_target_pairs={{0,1},{1,0},{2,3},{3,2},{4,5},{5,4},{6,7},{7,6},{8,9},{9,8},{10,11... | collective-permute-start | bytes 49160 | tf_op jit(solution)/shard_map/ppermute | solution.py:325
  25.4 38.5 %copy-start = (bf16[5,64,128]{2,1,0:T(8,128)(2,1)}, bf16[5,64,128]{2,1,0:T(8,128)(2,1)S(1)}, u32[]{:S(2)}) copy-start(bf16[5,64,128]{2,1,0:T(8,128)(2,1)S(1)} %collective-permute-done.other_ref) | copy-start | bytes 245764
  25.4 51.9 %copy-start.4 = (f32[2,128]{1,0:T(2,128)S(1)}, f32[2,128]{1,0:T(2,128)}, u32[]{:S(2)}) copy-start(f32[2,128]{1,0:T(2,128)} %gain_ref.1) | copy-start | bytes 3076
  25.4 51.9 %copy-start.5 = (f32[2,128]{1,0:T(2,128)S(1)}, f32[2,128]{1,0:T(2,128)}, u32[]{:S(2)}) copy-start(f32[2,128]{1,0:T(2,128)} %shift_ref.1) | copy-start | bytes 3076
  25.4 52.8 %copy-start.2 = (s32[8,512]{1,0:T(8,128)S(1)}, s32[8,512]{1,0:T(8,128)}, u32[]{:S(2)}) copy-start(s32[8,512]{1,0:T(8,128)} %param.13) | copy-start | bytes 49156
  63.9 15.6 %copy-start.3 = (bf16[64,128]{1,0:T(8,128)(2,1)S(1)}, bf16[64,128]{1,0:T(8,128)(2,1)}, u32[]{:S(2)}) copy-start(bf16[64,128]{1,0:T(8,128)(2,1)} %param.18) | copy-start | bytes 49156
  63.9 93.0 %all-to-all-start.1 = ((bf16[32,4,8,512]{3,2,1,0:T(8,128)(2,1)}), bf16[32,4,8,512]{3,2,1,0:T(8,128)(2,1)S(1)}, u32[]{:S(2)}, u32[]{:S(2)}) async-start(bf16[32,4,8,512]{3,2,1,0:T(8,128)(2,1)} %right.1), calls=%async_computation.1 | async-start | bytes 2097152 | tf_op jit(solution)/shard_map/all_to_all | solution.py:321
  156.8 84.4 %copy-start.1 = (bf16[32,4,8,512]{3,2,1,0:T(8,128)(2,1)}, bf16[32,4,8,512]{3,2,1,0:T(8,128)(2,1)S(1)}, u32[]{:S(2)}) copy-start(bf16[32,4,8,512]{3,2,1,0:T(8,128)(2,1)S(1)} %all-to-all-done.1.right_ref) | copy-start | bytes 3145732
  156.9 84.4 %all-to-all-start = ((bf16[32,4,8,512]{3,2,1,0:T(8,128)(2,1)}), bf16[32,4,8,512]{3,2,1,0:T(8,128)(2,1)S(1)}, u32[]{:S(2)}, u32[]{:S(2)}) async-start(bf16[32,4,8,512]{3,2,1,0:T(8,128)(2,1)} %left.1), calls=%async_computation | async-start | bytes 2097152 | tf_op jit(solution)/shard_map/all_to_all | solution.py:321
  162.9 78.4 %collective-permute-start.2 = (bf16[32,4,8,512]{3,2,1,0:T(8,128)(2,1)S(1)}, bf16[32,4,8,512]{3,2,1,0:T(8,128)(2,1)S(1)}, u32[]{:S(2)}, u32[]{:S(2)}) collective-permute-start(bf16[32,4,8,512]{3,2,1,0:T(8,128)(2,1)S(1)} %all-to-all-done.1.right_ref), channel_id=1, source_target_pairs={{0,1},{1,0},{2,3},{3,2},{4,5},{5,4},{6,7},{7,6},{8,9},{9,8},{10,11... | collective-permute-start | bytes 3145736 | tf_op jit(solution)/shard_map/ppermute | solution.py:338
  244.2 5.3 %copy-start.6 = (f32[64]{0:T(128)S(1)}, f32[64]{0:T(128)}, u32[]{:S(2)}) copy-start(f32[64]{0:T(128)} %param.21) | copy-start | bytes 772
  244.2 92.5 %all-to-all-start.2 = ((bf16[32,4,8,512]{3,2,1,0:T(8,128)(2,1)}), bf16[32,4,8,512]{3,2,1,0:T(8,128)(2,1)S(1)}, u32[]{:S(2)}, u32[]{:S(2)}) async-start(bf16[32,4,8,512]{3,2,1,0:T(8,128)(2,1)} %triangle.1), calls=%async_computation.2 | async-start | bytes 2097152 | tf_op jit(solution)/shard_map/all_to_all | solution.py:321
  393.0 1.9 collective-permute-start.3

commit v3 on v2

--- a/solution.py
+++ b/solution.py
@@ -308,7 +308,7 @@
     )(mask, own, *pinned(mine, other), targets, mask.reshape(1, length))
 
 
-LAG_NS = 35000
+LAG_NS = 39000
 
 
 def local(

time: 403 us -> 396 us (0.983); the launches traced: 398 us -> 395 us
  waiting for transfers between devices: 234 us -> 219 us
  starting transfers between devices: 45.5 us -> 51.3 us
    all_to_all x3, waiting for transfers between devices: 232 us -> 217 us  [local(): lax.all_to_all(v, 'row', split_axis=0, concat_axis=0, tiled=True)]
    all_to_all x3, starting transfers between devices: 24.7 us -> 30.4 us  [local(): lax.all_to_all(v, 'row', split_axis=0, concat_axis=0, tiled=True)]
  transfers between devices with their start and end apart: 7 -> 7, of which waited for: 4 -> 4; matrix products, arithmetic and copies ran while one was open for 1% -> 1% of each run, Pallas kernels for 13% -> 14%
where the time goes in v3:
time: 396 us; the launch traced here: 395 us
  waiting for transfers between devices  219 us (55%)
  Pallas kernels  66.7 us (17%)
  blocking collectives  53.7 us (14%)
  starting transfers between devices  51.3 us (13%)
    all_to_all x3, waiting for transfers between devices, local(): lax.all_to_all(v, 'row', split_axis=0, concat_axis=0, tiled=True)  217 us
    all_to_all x1, blocking collectives, local(): lax.all_to_all(v, 'row', split_axis=0, concat_axis=0, tiled=True)  53.7 us
    pallas_call x2, Pallas kernels, make_side(): pl.pallas_call(functools.partial(side_kernel, side, lag), in_specs=[pl.Bl...  45.9 us
    all_to_all x3, starting transfers between devices, local(): lax.all_to_all(v, 'row', split_axis=0, concat_axis=0, tiled=True)  30.4 us
    ppermute x1, starting transfers between devices, local(): w_other = swap(w_mine)  20.5 us
  transfers between devices with their start and end apart: 7, of which 4 were waited for; matrix products, arithmetic and copies ran while one was open for 1% of the time, Pallas kernels for 14%

profile of v3, /device:TPU:37, one launch (start us, length us, event | category | flops | bytes accessed | tf_op | source)
XLA Modules:
  0.0 395.3 jit_solution(8794671671761565679)
XLA Ops:
  0.6 20.5 %collective-permute-start = (bf16[5,64,128]{2,1,0:T(8,128)(2,1)}, bf16[5,64,128]{2,1,0:T(8,128)(2,1)S(1)}, u32[]{:S(2)}, u32[]{:S(2)}) collective-permute-start(bf16[5,64,128]{2,1,0:T(8,128)(2,1)} %bitcast.25), channel_id=1, source_target_pairs={{0,1},{1,0},{2,3},{3,2},{4,5},{5,4},{6,7},{7,6},{8,9},{9,8},{10,11... | collective-permute-start | bytes 245768 | tf_op jit(solution)/shard_map/ppermute | solution.py:324
  21.2 0.2 collective-permute-start.1
  21.3 4.1 %norm.1.normed_ref = bf16[8,512,128]{2,1,0:T(8,128)(2,1)} custom-call(bf16[8,512,128]{2,1,0:T(8,128)(2,1)} %pair_ref.1, f32[2,128]{1,0:T(2,128)} %gain_ref.1, f32[2,128]{1,0:T(2,128)} %shift_ref.1), custom_call_target="tpu_custom_call" | custom-call | flops 52428800 | bytes 2097152 | tf_op jit(solution)/shard_map/norm/pallas_call | solution.py:44
  25.4 0.0 collective-permute-done.other_ref
  25.4 0.0 copy-start.5
  25.4 0.0 copy-start.2
  25.4 42.4 %right.1 = bf16[32,4,8,512]{3,2,1,0:T(8,128)(2,1)} custom-call(s32[512]{0:T(512)} %mask_sref.5, bf16[8,512,128]{2,1,0:T(8,128)(2,1)} %norm.1.normed_ref, s32[1,512]{1,0:T(1,128)} %bitcast.32, bf16[5,64,128]{2,1,0:T(8,128)(2,1)} %bitcast.26, bf16[5,64,128]{2,1,0:T(8,128)(2,1)S(1)} %collective-permute-done.other_ref, f32[5,128]{1,0:T(8,128)} %b_ref.5), custom_call_target="tpu_custom_call" | custom-call | flops 268435456 | bytes 2097152 | tf_op jit(solution)/shard_map/right/pallas_call | solution.py:97
  67.9 0.0 collective-permute-done.1
  67.9 13.4 %all-to-all-start.1 = ((bf16[32,4,8,512]{3,2,1,0:T(8,128)(2,1)}), bf16[32,4,8,512]{3,2,1,0:T(8,128)(2,1)S(1)}, u32[]{:S(2)}, u32[]{:S(2)}) async-start(bf16[32,4,8,512]{3,2,1,0:T(8,128)(2,1)} %right.1), calls=%async_computation.1 | async-start | bytes 2097152 | tf_op jit(solution)/shard_map/all_to_all | solution.py:321
  81.3 0.1 stack.7
  81.4 0.1 stack.8
  81.5 0.7 copy.19
  82.2 0.4 reshape.51
  82.7 0.8 reshape.52.targets_ref
  83.5 0.6 copy.18
  84.1 3.4 left.1
  87.6 69.9 %all-to-all-done.1.right_ref = bf16[32,4,8,512]{3,2,1,0:T(8,128)(2,1)S(1)} async-done(((bf16[32,4,8,512]{3,2,1,0:T(8,128)(2,1)}), bf16[32,4,8,512]{3,2,1,0:T(8,128)(2,1)S(1)}, u32[]{:S(2)}, u32[]{:S(2)}) %all-to-all-start.1) | async-done | bytes 1048608 | tf_op jit(solution)/shard_map/all_to_all | solution.py:321
  157.5 11.6 %all-to-all-start = ((bf16[32,4,8,512]{3,2,1,0:T(8,128)(2,1)}), bf16[32,4,8,512]{3,2,1,0:T(8,128)(2,1)S(1)}, u32[]{:S(2)}, u32[]{:S(2)}) async-start(bf16[32,4,8,512]{3,2,1,0:T(8,128)(2,1)} %left.1), calls=%async_computation | async-start | bytes 2097152 | tf_op jit(solution)/shard_map/all_to_all | solution.py:321
  169.1 0.1 collective-permute-start.2
  169.2 71.4 %all-to-all-done.left_ref = bf16[32,4,8,512]{3,2,1,0:T(8,128)(2,1)S(1)} async-done(((bf16[32,4,8,512]{3,2,1,0:T(8,128)(2,1)}), bf16[32,4,8,512]{3,2,1,0:T(8,128)(2,1)S(1)}, u32[]{:S(2)}, u32[]{:S(2)}) %all-to-all-start) | async-done | bytes 1048608 | tf_op jit(solution)/shard_map/all_to_all | solution.py:321
  240.6 0.0 collective-permute-done.2.other_ref
  240.6 2.9 triangle.1
  243.6 5.4 %all-to-all-start.2 = ((bf16[32,4,8,512]{3,2,1,0:T(8,128)(2,1)}), bf16[32,4,8,512]{3,2,1,0:T(8,128)(2,1)S(1)}, u32[]{:S(2)}, u32[]{:S(2)}) async-start(bf16[32,4,8,512]{3,2,1,0:T(8,128)(2,1)} %triangle.1), calls=%async_computation.2 | async-start | bytes 2097152 | tf_op jit(solution)/shard_map/all_to_all | solution.py:321
  249.0 0.7 copy.20.headbt_ref
  249.7 0.6 maximum_bitcast_fusion.1.headb_ref
  250.3 5.2 %gate.1 = f32[8,512,128]{2,1,0:T(8,128)} custom-call(bf16[8,512,128]{2,1,0:T(8,128)(2,1)} %norm.1.normed_ref, bf16[5,64,128]{2,1,0:T(8,128)(2,1)} %bitcast.28, bf16[5,64,128]{2,1,0:T(8,128)(2,1)} %copy-done, f32[5,128]{1,0:T(8,128)} %b_ref.5), custom_call_target="tpu_custom_call" | custom-call | flops 134217728 | bytes 3145728 | tf_op jit(solution)/shard_map/gate/pallas_call | solution.py:118
  255.5 75.6 %all-to-all-done.2 = bf16[32,4,8,512]{3,2,1,0:T(8,128)(2,1)S(1)} async-done(((bf16[32,4,8,512]{3,2,1,0:T(8,128)(2,1)}), bf16[32,4,8,512]{3,2,1,0:T(8,128)(2,1)S(1)}, u32[]{:S(2)}, u32[]{:S(2)}) %all-to-all-start.2) | async-done | bytes 1048608 | tf_op jit(solution)/shard_map/all_to_all | solution.py:321
  331.1 5.5 %finish.1 = (bf16[8,32,2,8,128]{4,3,2,1,0:T(8,128)(2,1)}, bf16[32,8,8,128]{3,2,1,0:T(8,128)(2,1)}, f32[4,512,128]{2,1,0:T(8,128)}) custom-call(bf16[128,8,512]{2,1,0:T(8,128)(2,1)S(1)} %bitcast.21, f32[8,32,2,8,128]{4,3,2,1,0:T(8,128)} %bitcast.22, bf16[8,32,2,8,128]{4,3,2,1,0:T(8,128)(2,1)} %bitcast.23, bf16[128,128]{1,0:T(8,128)(2,1)} %bitcast.30, ...), custom_call_target="tpu_custom_call" | custom-call | tf_op jit(solution)/shard_map/finish/pallas_call | solution.py:217
  336.6 53.7 %all_to_all.20.mine_ref = bf16[32,8,8,128]{3,2,1,0:T(8,128)(2,1)S(1)} all-to-all(bf16[32,8,8,128]{3,2,1,0:T(8,128)(2,1)} %get-tuple-element.18), channel_id=1, replica_groups=mesh['ga'=4,'row'=32,'col'=2] {'row'}, dimensions={0} | all-to-all | bytes 1048576 | tf_op jit(solution)/shard_map/all_to_all | solution.py:321
  390.3 0.0 collective-permute-start.3
  390.3 1.9 collective-permute-done.3.other_ref
  392.2 3.1 loss.1
  (17 shorter events, 0.1 us)
Async XLA Ops:
  0.6 24.8 %collective-permute-start = (bf16[5,64,128]{2,1,0:T(8,128)(2,1)}, bf16[5,64,128]{2,1,0:T(8,128)(2,1)S(1)}, u32[]{:S(2)}, u32[]{:S(2)}) collective-permute-start(bf16[5,64,128]{2,1,0:T(8,128)(2,1)} %bitcast.25), channel_id=1, source_target_pairs={{0,1},{1,0},{2,3},{3,2},{4,5},{5,4},{6,7},{7,6},{8,9},{9,8},{10,11... | collective-permute-start | bytes 245768 | tf_op jit(solution)/shard_map/ppermute | solution.py:324
  21.2 46.7 %collective-permute-start.1 = (bf16[64,128]{1,0:T(8,128)(2,1)}, bf16[64,128]{1,0:T(8,128)(2,1)S(1)}, u32[]{:S(2)}, u32[]{:S(2)}) collective-permute-start(bf16[64,128]{1,0:T(8,128)(2,1)} %param.18), channel_id=1, source_target_pairs={{0,1},{1,0},{2,3},{3,2},{4,5},{5,4},{6,7},{7,6},{8,9},{9,8},{10,11... | collective-permute-start | bytes 49160 | tf_op jit(solution)/shard_map/ppermute | solution.py:325
  25.4 42.5 %copy-start = (bf16[5,64,128]{2,1,0:T(8,128)(2,1)}, bf16[5,64,128]{2,1,0:T(8,128)(2,1)S(1)}, u32[]{:S(2)}) copy-start(bf16[5,64,128]{2,1,0:T(8,128)(2,1)S(1)} %collective-permute-done.other_ref) | copy-start | bytes 245764
  25.4 55.9 %copy-start.4 = (f32[2,128]{1,0:T(2,128)S(1)}, f32[2,128]{1,0:T(2,128)}, u32[]{:S(2)}) copy-start(f32[2,128]{1,0:T(2,128)} %gain_ref.1) | copy-start | bytes 3076
  25.4 55.9 %copy-start.5 = (f32[2,128]{1,0:T(2,128)S(1)}, f32[2,128]{1,0:T(2,128)}, u32[]{:S(2)}) copy-start(f32[2,128]{1,0:T(2,128)} %shift_ref.1) | copy-start | bytes 3076
  25.4 56.8 %copy-start.2 = (s32[8,512]{1,0:T(8,128)S(1)}, s32[8,512]{1,0:T(8,128)}, u32[]{:S(2)}) copy-start(s32[8,512]{1,0:T(8,128)} %param.13) | copy-start | bytes 49156
  67.9 15.6 %copy-start.3 = (bf16[64,128]{1,0:T(8,128)(2,1)S(1)}, bf16[64,128]{1,0:T(8,128)(2,1)}, u32[]{:S(2)}) copy-start(bf16[64,128]{1,0:T(8,128)(2,1)} %param.18) | copy-start | bytes 49156
  67.9 89.6 %all-to-all-start.1 = ((bf16[32,4,8,512]{3,2,1,0:T(8,128)(2,1)}), bf16[32,4,8,512]{3,2,1,0:T(8,128)(2,1)S(1)}, u32[]{:S(2)}, u32[]{:S(2)}) async-start(bf16[32,4,8,512]{3,2,1,0:T(8,128)(2,1)} %right.1), calls=%async_computation.1 | async-start | bytes 2097152 | tf_op jit(solution)/shard_map/all_to_all | solution.py:321
  157.5 83.2 %copy-start.1 = (bf16[32,4,8,512]{3,2,1,0:T(8,128)(2,1)}, bf16[32,4,8,512]{3,2,1,0:T(8,128)(2,1)S(1)}, u32[]{:S(2)}) copy-start(bf16[32,4,8,512]{3,2,1,0:T(8,128)(2,1)S(1)} %all-to-all-done.1.right_ref) | copy-start | bytes 3145732
  157.5 83.1 %all-to-all-start = ((bf16[32,4,8,512]{3,2,1,0:T(8,128)(2,1)}), bf16[32,4,8,512]{3,2,1,0:T(8,128)(2,1)S(1)}, u32[]{:S(2)}, u32[]{:S(2)}) async-start(bf16[32,4,8,512]{3,2,1,0:T(8,128)(2,1)} %left.1), calls=%async_computation | async-start | bytes 2097152 | tf_op jit(solution)/shard_map/all_to_all | solution.py:321
  169.1 71.5 %collective-permute-start.2 = (bf16[32,4,8,512]{3,2,1,0:T(8,128)(2,1)S(1)}, bf16[32,4,8,512]{3,2,1,0:T(8,128)(2,1)S(1)}, u32[]{:S(2)}, u32[]{:S(2)}) collective-permute-start(bf16[32,4,8,512]{3,2,1,0:T(8,128)(2,1)S(1)} %all-to-all-done.1.right_ref), channel_id=1, source_target_pairs={{0,1},{1,0},{2,3},{3,2},{4,5},{5,4},{6,7},{7,6},{8,9},{9,8},{10,11... | collective-permute-start | bytes 3145736 | tf_op jit(solution)/shard_map/ppermute | solution.py:338
  243.6 5.4 %copy-start.6 = (f32[64]{0:T(128)S(1)}, f32[64]{0:T(128)}, u32[]{:S(2)}) copy-start(f32[64]{0:T(128)} %param.21) | copy-start | bytes 772
  243.6 87.5 %all-to-all-start.2 = ((bf16[32,4,8,512]{3,2,1,0:T(8,128)(2,1)}), bf16[32,4,8,512]{3,2,1,0:T(8,128)(2,1)S(1)}, u32[]{:S(2)}, u32[]{:S(2)}) async-start(bf16[32,4,8,512]{3,2,1,0:T(8,128)(2,1)} %triangle.1), calls=%async_computation.2 | async-start | bytes 2097152 | tf_op jit(solution)/shard_map/all_to_all | solution.py:321
  390.3 1.9 collective-permute-start.3

commit v4 on v3

--- a/solution.py
+++ b/solution.py
@@ -308,7 +308,7 @@
     )(mask, own, *pinned(mine, other), targets, mask.reshape(1, length))
 
 
-LAG_NS = 39000
+LAG_NS = 38000
 
 
 def local(

time: 396 us -> 389 us (0.982)
  starting transfers between devices: 51.3 us -> 59.1 us
  waiting for transfers between devices: 219 us -> 212 us
  blocking collectives: 53.7 us -> 47.3 us
    all_to_all x3, starting transfers between devices: 30.4 us -> 38.3 us  [local(): lax.all_to_all(v, 'row', split_axis=0, concat_axis=0, tiled=True)]
    all_to_all x3, waiting for transfers between devices: 217 us -> 210 us  [local(): lax.all_to_all(v, 'row', split_axis=0, concat_axis=0, tiled=True)]
    all_to_all x1, blocking collectives: 53.7 us -> 47.3 us  [local(): lax.all_to_all(v, 'row', split_axis=0, concat_axis=0, tiled=True)]
where the time goes in v4:
time: 389 us
  waiting for transfers between devices  212 us (54%)
  Pallas kernels  65.7 us (17%)
  starting transfers between devices  59.1 us (15%)
  blocking collectives  47.3 us (12%)
    all_to_all x3, waiting for transfers between devices, local(): lax.all_to_all(v, 'row', split_axis=0, concat_axis=0, tiled=True)  210 us
    all_to_all x1, blocking collectives, local(): lax.all_to_all(v, 'row', split_axis=0, concat_axis=0, tiled=True)  47.3 us
    pallas_call x2, Pallas kernels, make_side(): pl.pallas_call(functools.partial(side_kernel, side, lag), in_specs=[pl.Bl...  44.9 us
    all_to_all x3, starting transfers between devices, local(): lax.all_to_all(v, 'row', split_axis=0, concat_axis=0, tiled=True)  38.3 us
    ppermute x1, starting transfers between devices, local(): w_other = swap(w_mine)  20.5 us
  transfers between devices with their start and end apart: 7, of which 4 were waited for; matrix products, arithmetic and copies ran while one was open for 1% of the time, Pallas kernels for 14%

profile of v4, /device:TPU:37, one launch (start us, length us, event | category | flops | bytes accessed | tf_op | source)
XLA Modules:
  0.0 388.6 jit_solution(17203027580038477063)
XLA Ops:
  0.6 20.5 %collective-permute-start = (bf16[5,64,128]{2,1,0:T(8,128)(2,1)}, bf16[5,64,128]{2,1,0:T(8,128)(2,1)S(1)}, u32[]{:S(2)}, u32[]{:S(2)}) collective-permute-start(bf16[5,64,128]{2,1,0:T(8,128)(2,1)} %bitcast.25), channel_id=1, source_target_pairs={{0,1},{1,0},{2,3},{3,2},{4,5},{5,4},{6,7},{7,6},{8,9},{9,8},{10,11... | collective-permute-start | bytes 245768 | tf_op jit(solution)/shard_map/ppermute | solution.py:324
  21.2 0.2 collective-permute-start.1
  21.3 4.1 %norm.1.normed_ref = bf16[8,512,128]{2,1,0:T(8,128)(2,1)} custom-call(bf16[8,512,128]{2,1,0:T(8,128)(2,1)} %pair_ref.1, f32[2,128]{1,0:T(2,128)} %gain_ref.1, f32[2,128]{1,0:T(2,128)} %shift_ref.1), custom_call_target="tpu_custom_call" | custom-call | flops 52428800 | bytes 2097152 | tf_op jit(solution)/shard_map/norm/pallas_call | solution.py:44
  25.4 0.0 collective-permute-done.other_ref
  25.4 0.0 copy-start.5
  25.4 0.0 copy-start.2
  25.4 41.4 %right.1 = bf16[32,4,8,512]{3,2,1,0:T(8,128)(2,1)} custom-call(s32[512]{0:T(512)} %mask_sref.5, bf16[8,512,128]{2,1,0:T(8,128)(2,1)} %norm.1.normed_ref, s32[1,512]{1,0:T(1,128)} %bitcast.32, bf16[5,64,128]{2,1,0:T(8,128)(2,1)} %bitcast.26, bf16[5,64,128]{2,1,0:T(8,128)(2,1)S(1)} %collective-permute-done.other_ref, f32[5,128]{1,0:T(8,128)} %b_ref.5), custom_call_target="tpu_custom_call" | custom-call | flops 268435456 | bytes 2097152 | tf_op jit(solution)/shard_map/right/pallas_call | solution.py:97
  66.9 0.0 collective-permute-done.1
  66.9 13.4 %all-to-all-start.1 = ((bf16[32,4,8,512]{3,2,1,0:T(8,128)(2,1)}), bf16[32,4,8,512]{3,2,1,0:T(8,128)(2,1)S(1)}, u32[]{:S(2)}, u32[]{:S(2)}) async-start(bf16[32,4,8,512]{3,2,1,0:T(8,128)(2,1)} %right.1), calls=%async_computation.1 | async-start | bytes 2097152 | tf_op jit(solution)/shard_map/all_to_all | solution.py:321
  80.3 0.1 stack.7
  80.4 0.1 stack.8
  80.5 0.7 copy.19
  81.3 0.4 reshape.51
  81.7 0.8 reshape.52.targets_ref
  82.5 0.6 copy.18
  83.1 3.4 left.1
  86.6 69.8 %all-to-all-done.1.right_ref = bf16[32,4,8,512]{3,2,1,0:T(8,128)(2,1)S(1)} async-done(((bf16[32,4,8,512]{3,2,1,0:T(8,128)(2,1)}), bf16[32,4,8,512]{3,2,1,0:T(8,128)(2,1)S(1)}, u32[]{:S(2)}, u32[]{:S(2)}) %all-to-all-start.1) | async-done | bytes 1048608 | tf_op jit(solution)/shard_map/all_to_all | solution.py:321
  156.3 14.5 %all-to-all-start = ((bf16[32,4,8,512]{3,2,1,0:T(8,128)(2,1)}), bf16[32,4,8,512]{3,2,1,0:T(8,128)(2,1)S(1)}, u32[]{:S(2)}, u32[]{:S(2)}) async-start(bf16[32,4,8,512]{3,2,1,0:T(8,128)(2,1)} %left.1), calls=%async_computation | async-start | bytes 2097152 | tf_op jit(solution)/shard_map/all_to_all | solution.py:321
  170.9 0.1 collective-permute-start.2
  171.0 72.7 %all-to-all-done.left_ref = bf16[32,4,8,512]{3,2,1,0:T(8,128)(2,1)S(1)} async-done(((bf16[32,4,8,512]{3,2,1,0:T(8,128)(2,1)}), bf16[32,4,8,512]{3,2,1,0:T(8,128)(2,1)S(1)}, u32[]{:S(2)}, u32[]{:S(2)}) %all-to-all-start) | async-done | bytes 1048608 | tf_op jit(solution)/shard_map/all_to_all | solution.py:321
  243.7 0.0 collective-permute-done.2.other_ref
  243.7 2.9 triangle.1
  246.6 10.3 %all-to-all-start.2 = ((bf16[32,4,8,512]{3,2,1,0:T(8,128)(2,1)}), bf16[32,4,8,512]{3,2,1,0:T(8,128)(2,1)S(1)}, u32[]{:S(2)}, u32[]{:S(2)}) async-start(bf16[32,4,8,512]{3,2,1,0:T(8,128)(2,1)} %triangle.1), calls=%async_computation.2 | async-start | bytes 2097152 | tf_op jit(solution)/shard_map/all_to_all | solution.py:321
  257.0 0.7 copy.20.headbt_ref
  257.7 0.6 maximum_bitcast_fusion.1.headb_ref
  258.2 5.2 %gate.1 = f32[8,512,128]{2,1,0:T(8,128)} custom-call(bf16[8,512,128]{2,1,0:T(8,128)(2,1)} %norm.1.normed_ref, bf16[5,64,128]{2,1,0:T(8,128)(2,1)} %bitcast.28, bf16[5,64,128]{2,1,0:T(8,128)(2,1)} %copy-done, f32[5,128]{1,0:T(8,128)} %b_ref.5), custom_call_target="tpu_custom_call" | custom-call | flops 134217728 | bytes 3145728 | tf_op jit(solution)/shard_map/gate/pallas_call | solution.py:118
  263.4 67.3 %all-to-all-done.2 = bf16[32,4,8,512]{3,2,1,0:T(8,128)(2,1)S(1)} async-done(((bf16[32,4,8,512]{3,2,1,0:T(8,128)(2,1)}), bf16[32,4,8,512]{3,2,1,0:T(8,128)(2,1)S(1)}, u32[]{:S(2)}, u32[]{:S(2)}) %all-to-all-start.2) | async-done | bytes 1048608 | tf_op jit(solution)/shard_map/all_to_all | solution.py:321
  330.7 5.5 %finish.1 = (bf16[8,32,2,8,128]{4,3,2,1,0:T(8,128)(2,1)}, bf16[32,8,8,128]{3,2,1,0:T(8,128)(2,1)}, f32[4,512,128]{2,1,0:T(8,128)}) custom-call(bf16[128,8,512]{2,1,0:T(8,128)(2,1)S(1)} %bitcast.21, f32[8,32,2,8,128]{4,3,2,1,0:T(8,128)} %bitcast.22, bf16[8,32,2,8,128]{4,3,2,1,0:T(8,128)(2,1)} %bitcast.23, bf16[128,128]{1,0:T(8,128)(2,1)} %bitcast.30, ...), custom_call_target="tpu_custom_call" | custom-call | tf_op jit(solution)/shard_map/finish/pallas_call | solution.py:217
  336.2 47.3 %all_to_all.20.mine_ref = bf16[32,8,8,128]{3,2,1,0:T(8,128)(2,1)S(1)} all-to-all(bf16[32,8,8,128]{3,2,1,0:T(8,128)(2,1)} %get-tuple-element.18), channel_id=1, replica_groups=mesh['ga'=4,'row'=32,'col'=2] {'row'}, dimensions={0} | all-to-all | bytes 1048576 | tf_op jit(solution)/shard_map/all_to_all | solution.py:321
  383.6 0.0 collective-permute-start.3
  383.6 1.9 collective-permute-done.3.other_ref
  385.5 3.1 loss.1
  (17 shorter events, 0.1 us)
Async XLA Ops:
  0.6 24.8 %collective-permute-start = (bf16[5,64,128]{2,1,0:T(8,128)(2,1)}, bf16[5,64,128]{2,1,0:T(8,128)(2,1)S(1)}, u32[]{:S(2)}, u32[]{:S(2)}) collective-permute-start(bf16[5,64,128]{2,1,0:T(8,128)(2,1)} %bitcast.25), channel_id=1, source_target_pairs={{0,1},{1,0},{2,3},{3,2},{4,5},{5,4},{6,7},{7,6},{8,9},{9,8},{10,11... | collective-permute-start | bytes 245768 | tf_op jit(solution)/shard_map/ppermute | solution.py:324
  21.2 45.7 %collective-permute-start.1 = (bf16[64,128]{1,0:T(8,128)(2,1)}, bf16[64,128]{1,0:T(8,128)(2,1)S(1)}, u32[]{:S(2)}, u32[]{:S(2)}) collective-permute-start(bf16[64,128]{1,0:T(8,128)(2,1)} %param.18), channel_id=1, source_target_pairs={{0,1},{1,0},{2,3},{3,2},{4,5},{5,4},{6,7},{7,6},{8,9},{9,8},{10,11... | collective-permute-start | bytes 49160 | tf_op jit(solution)/shard_map/ppermute | solution.py:325
  25.4 41.5 %copy-start = (bf16[5,64,128]{2,1,0:T(8,128)(2,1)}, bf16[5,64,128]{2,1,0:T(8,128)(2,1)S(1)}, u32[]{:S(2)}) copy-start(bf16[5,64,128]{2,1,0:T(8,128)(2,1)S(1)} %collective-permute-done.other_ref) | copy-start | bytes 245764
  25.4 54.9 %copy-start.4 = (f32[2,128]{1,0:T(2,128)S(1)}, f32[2,128]{1,0:T(2,128)}, u32[]{:S(2)}) copy-start(f32[2,128]{1,0:T(2,128)} %gain_ref.1) | copy-start | bytes 3076
  25.4 54.9 %copy-start.5 = (f32[2,128]{1,0:T(2,128)S(1)}, f32[2,128]{1,0:T(2,128)}, u32[]{:S(2)}) copy-start(f32[2,128]{1,0:T(2,128)} %shift_ref.1) | copy-start | bytes 3076
  25.4 55.8 %copy-start.2 = (s32[8,512]{1,0:T(8,128)S(1)}, s32[8,512]{1,0:T(8,128)}, u32[]{:S(2)}) copy-start(s32[8,512]{1,0:T(8,128)} %param.13) | copy-start | bytes 49156
  66.9 15.6 %copy-start.3 = (bf16[64,128]{1,0:T(8,128)(2,1)S(1)}, bf16[64,128]{1,0:T(8,128)(2,1)}, u32[]{:S(2)}) copy-start(bf16[64,128]{1,0:T(8,128)(2,1)} %param.18) | copy-start | bytes 49156
  66.9 89.4 %all-to-all-start.1 = ((bf16[32,4,8,512]{3,2,1,0:T(8,128)(2,1)}), bf16[32,4,8,512]{3,2,1,0:T(8,128)(2,1)S(1)}, u32[]{:S(2)}, u32[]{:S(2)}) async-start(bf16[32,4,8,512]{3,2,1,0:T(8,128)(2,1)} %right.1), calls=%async_computation.1 | async-start | bytes 2097152 | tf_op jit(solution)/shard_map/all_to_all | solution.py:321
  156.3 87.3 %copy-start.1 = (bf16[32,4,8,512]{3,2,1,0:T(8,128)(2,1)}, bf16[32,4,8,512]{3,2,1,0:T(8,128)(2,1)S(1)}, u32[]{:S(2)}) copy-start(bf16[32,4,8,512]{3,2,1,0:T(8,128)(2,1)S(1)} %all-to-all-done.1.right_ref) | copy-start | bytes 3145732
  156.3 87.3 %all-to-all-start = ((bf16[32,4,8,512]{3,2,1,0:T(8,128)(2,1)}), bf16[32,4,8,512]{3,2,1,0:T(8,128)(2,1)S(1)}, u32[]{:S(2)}, u32[]{:S(2)}) async-start(bf16[32,4,8,512]{3,2,1,0:T(8,128)(2,1)} %left.1), calls=%async_computation | async-start | bytes 2097152 | tf_op jit(solution)/shard_map/all_to_all | solution.py:321
  170.9 72.8 %collective-permute-start.2 = (bf16[32,4,8,512]{3,2,1,0:T(8,128)(2,1)S(1)}, bf16[32,4,8,512]{3,2,1,0:T(8,128)(2,1)S(1)}, u32[]{:S(2)}, u32[]{:S(2)}) collective-permute-start(bf16[32,4,8,512]{3,2,1,0:T(8,128)(2,1)S(1)} %all-to-all-done.1.right_ref), channel_id=1, source_target_pairs={{0,1},{1,0},{2,3},{3,2},{4,5},{5,4},{6,7},{7,6},{8,9},{9,8},{10,11... | collective-permute-start | bytes 3145736 | tf_op jit(solution)/shard_map/ppermute | solution.py:338
  246.6 10.3 %copy-start.6 = (f32[64]{0:T(128)S(1)}, f32[64]{0:T(128)}, u32[]{:S(2)}) copy-start(f32[64]{0:T(128)} %param.21) | copy-start | bytes 772
  246.6 84.1 %all-to-all-start.2 = ((bf16[32,4,8,512]{3,2,1,0:T(8,128)(2,1)}), bf16[32,4,8,512]{3,2,1,0:T(8,128)(2,1)S(1)}, u32[]{:S(2)}, u32[]{:S(2)}) async-start(bf16[32,4,8,512]{3,2,1,0:T(8,128)(2,1)} %triangle.1), calls=%async_computation.2 | async-start | bytes 2097152 | tf_op jit(solution)/shard_map/all_to_all | solution.py:321
  383.6 1.9 collective-permute-start.3

commit v5 on v4

--- a/solution.py
+++ b/solution.py
@@ -43,9 +43,9 @@
     rows, length, chans = pair.shape
     return pl.pallas_call(
         norm_kernel,
-        grid=(rows // 2,),
+        grid=(rows // 4,),
         in_specs=[
-            pl.BlockSpec((2, length, chans), lambda r: (r, 0, 0)),
+            pl.BlockSpec((4, length, chans), lambda r: (r, 0, 0)),
             whole(*gain.shape),
             whole(*shift.shape),
         ],

time: 389 us -> 388 us (level)
  no operation moved by 1% of the time
where the time goes in v5:
time: 388 us; the launch traced here: 387 us
  waiting for transfers between devices  212 us (55%)
  Pallas kernels  64.8 us (17%)
  starting transfers between devices  59.1 us (15%)
  blocking collectives  46.8 us (12%)
    all_to_all x3, waiting for transfers between devices, local(): lax.all_to_all(v, 'row', split_axis=0, concat_axis=0, tiled=True)  210 us
    all_to_all x1, blocking collectives, local(): lax.all_to_all(v, 'row', split_axis=0, concat_axis=0, tiled=True)  46.8 us
    pallas_call x2, Pallas kernels, make_side(): pl.pallas_call(functools.partial(side_kernel, side, lag), in_specs=[pl.Bl...  44.9 us
    all_to_all x3, starting transfers between devices, local(): lax.all_to_all(v, 'row', split_axis=0, concat_axis=0, tiled=True)  38.2 us
    ppermute x1, starting transfers between devices, local(): w_other = swap(w_mine)  20.5 us
  transfers between devices with their start and end apart: 7, of which 4 were waited for; matrix products, arithmetic and copies ran while one was open for 1% of the time, Pallas kernels for 14%

profile of v5, /device:TPU:37, one launch (start us, length us, event | category | flops | bytes accessed | tf_op | source)
XLA Modules:
  0.0 387.0 jit_solution(16483218933986138474)
XLA Ops:
  0.6 20.5 %collective-permute-start = (bf16[5,64,128]{2,1,0:T(8,128)(2,1)}, bf16[5,64,128]{2,1,0:T(8,128)(2,1)S(1)}, u32[]{:S(2)}, u32[]{:S(2)}) collective-permute-start(bf16[5,64,128]{2,1,0:T(8,128)(2,1)} %bitcast.25), channel_id=1, source_target_pairs={{0,1},{1,0},{2,3},{3,2},{4,5},{5,4},{6,7},{7,6},{8,9},{9,8},{10,11... | collective-permute-start | bytes 245768 | tf_op jit(solution)/shard_map/ppermute | solution.py:324
  21.2 0.2 collective-permute-start.1
  21.3 3.1 norm.1.normed_ref
  24.4 0.0 collective-permute-done.other_ref
  24.4 0.0 copy-start.5
  24.4 0.0 copy-start.2
  24.5 41.4 %right.1 = bf16[32,4,8,512]{3,2,1,0:T(8,128)(2,1)} custom-call(s32[512]{0:T(512)} %mask_sref.5, bf16[8,512,128]{2,1,0:T(8,128)(2,1)} %norm.1.normed_ref, s32[1,512]{1,0:T(1,128)} %bitcast.32, bf16[5,64,128]{2,1,0:T(8,128)(2,1)} %bitcast.26, bf16[5,64,128]{2,1,0:T(8,128)(2,1)S(1)} %collective-permute-done.other_ref, f32[5,128]{1,0:T(8,128)} %b_ref.5), custom_call_target="tpu_custom_call" | custom-call | flops 268435456 | bytes 2097152 | tf_op jit(solution)/shard_map/right/pallas_call | solution.py:97
  65.9 0.0 collective-permute-done.1
  65.9 13.4 %all-to-all-start.1 = ((bf16[32,4,8,512]{3,2,1,0:T(8,128)(2,1)}), bf16[32,4,8,512]{3,2,1,0:T(8,128)(2,1)S(1)}, u32[]{:S(2)}, u32[]{:S(2)}) async-start(bf16[32,4,8,512]{3,2,1,0:T(8,128)(2,1)} %right.1), calls=%async_computation.1 | async-start | bytes 2097152 | tf_op jit(solution)/shard_map/all_to_all | solution.py:321
  79.4 0.1 stack.7
  79.4 0.1 stack.8
  79.5 0.7 copy.19
  80.3 0.4 reshape.51
  80.7 0.8 reshape.52.targets_ref
  81.5 0.6 copy.18
  82.1 3.4 left.1
  85.6 69.8 %all-to-all-done.1.right_ref = bf16[32,4,8,512]{3,2,1,0:T(8,128)(2,1)S(1)} async-done(((bf16[32,4,8,512]{3,2,1,0:T(8,128)(2,1)}), bf16[32,4,8,512]{3,2,1,0:T(8,128)(2,1)S(1)}, u32[]{:S(2)}, u32[]{:S(2)}) %all-to-all-start.1) | async-done | bytes 1048608 | tf_op jit(solution)/shard_map/all_to_all | solution.py:321
  155.3 14.5 %all-to-all-start = ((bf16[32,4,8,512]{3,2,1,0:T(8,128)(2,1)}), bf16[32,4,8,512]{3,2,1,0:T(8,128)(2,1)S(1)}, u32[]{:S(2)}, u32[]{:S(2)}) async-start(bf16[32,4,8,512]{3,2,1,0:T(8,128)(2,1)} %left.1), calls=%async_computation | async-start | bytes 2097152 | tf_op jit(solution)/shard_map/all_to_all | solution.py:321
  169.9 0.1 collective-permute-start.2
  170.0 72.7 %all-to-all-done.left_ref = bf16[32,4,8,512]{3,2,1,0:T(8,128)(2,1)S(1)} async-done(((bf16[32,4,8,512]{3,2,1,0:T(8,128)(2,1)}), bf16[32,4,8,512]{3,2,1,0:T(8,128)(2,1)S(1)}, u32[]{:S(2)}, u32[]{:S(2)}) %all-to-all-start) | async-done | bytes 1048608 | tf_op jit(solution)/shard_map/all_to_all | solution.py:321
  242.7 0.0 collective-permute-done.2.other_ref
  242.7 3.0 triangle.1
  245.7 10.3 %all-to-all-start.2 = ((bf16[32,4,8,512]{3,2,1,0:T(8,128)(2,1)}), bf16[32,4,8,512]{3,2,1,0:T(8,128)(2,1)S(1)}, u32[]{:S(2)}, u32[]{:S(2)}) async-start(bf16[32,4,8,512]{3,2,1,0:T(8,128)(2,1)} %triangle.1), calls=%async_computation.2 | async-start | bytes 2097152 | tf_op jit(solution)/shard_map/all_to_all | solution.py:321
  256.0 0.7 copy.20.headbt_ref
  256.7 0.6 maximum_bitcast_fusion.1.headb_ref
  257.3 5.2 %gate.1 = f32[8,512,128]{2,1,0:T(8,128)} custom-call(bf16[8,512,128]{2,1,0:T(8,128)(2,1)} %norm.1.normed_ref, bf16[5,64,128]{2,1,0:T(8,128)(2,1)} %bitcast.28, bf16[5,64,128]{2,1,0:T(8,128)(2,1)} %copy-done, f32[5,128]{1,0:T(8,128)} %b_ref.5), custom_call_target="tpu_custom_call" | custom-call | flops 134217728 | bytes 3145728 | tf_op jit(solution)/shard_map/gate/pallas_call | solution.py:118
  262.5 67.2 %all-to-all-done.2 = bf16[32,4,8,512]{3,2,1,0:T(8,128)(2,1)S(1)} async-done(((bf16[32,4,8,512]{3,2,1,0:T(8,128)(2,1)}), bf16[32,4,8,512]{3,2,1,0:T(8,128)(2,1)S(1)}, u32[]{:S(2)}, u32[]{:S(2)}) %all-to-all-start.2) | async-done | bytes 1048608 | tf_op jit(solution)/shard_map/all_to_all | solution.py:321
  329.7 5.5 %finish.1 = (bf16[8,32,2,8,128]{4,3,2,1,0:T(8,128)(2,1)}, bf16[32,8,8,128]{3,2,1,0:T(8,128)(2,1)}, f32[4,512,128]{2,1,0:T(8,128)}) custom-call(bf16[128,8,512]{2,1,0:T(8,128)(2,1)S(1)} %bitcast.21, f32[8,32,2,8,128]{4,3,2,1,0:T(8,128)} %bitcast.22, bf16[8,32,2,8,128]{4,3,2,1,0:T(8,128)(2,1)} %bitcast.23, bf16[128,128]{1,0:T(8,128)(2,1)} %bitcast.30, ...), custom_call_target="tpu_custom_call" | custom-call | tf_op jit(solution)/shard_map/finish/pallas_call | solution.py:217
  335.2 46.8 %all_to_all.20.mine_ref = bf16[32,8,8,128]{3,2,1,0:T(8,128)(2,1)S(1)} all-to-all(bf16[32,8,8,128]{3,2,1,0:T(8,128)(2,1)} %get-tuple-element.18), channel_id=1, replica_groups=mesh['ga'=4,'row'=32,'col'=2] {'row'}, dimensions={0} | all-to-all | bytes 1048576 | tf_op jit(solution)/shard_map/all_to_all | solution.py:321
  382.0 0.0 collective-permute-start.3
  382.1 1.9 collective-permute-done.3.other_ref
  384.0 3.1 loss.1
  (17 shorter events, 0.1 us)
Async XLA Ops:
  0.6 23.8 %collective-permute-start = (bf16[5,64,128]{2,1,0:T(8,128)(2,1)}, bf16[5,64,128]{2,1,0:T(8,128)(2,1)S(1)}, u32[]{:S(2)}, u32[]{:S(2)}) collective-permute-start(bf16[5,64,128]{2,1,0:T(8,128)(2,1)} %bitcast.25), channel_id=1, source_target_pairs={{0,1},{1,0},{2,3},{3,2},{4,5},{5,4},{6,7},{7,6},{8,9},{9,8},{10,11... | collective-permute-start | bytes 245768 | tf_op jit(solution)/shard_map/ppermute | solution.py:324
  21.2 44.7 %collective-permute-start.1 = (bf16[64,128]{1,0:T(8,128)(2,1)}, bf16[64,128]{1,0:T(8,128)(2,1)S(1)}, u32[]{:S(2)}, u32[]{:S(2)}) collective-permute-start(bf16[64,128]{1,0:T(8,128)(2,1)} %param.18), channel_id=1, source_target_pairs={{0,1},{1,0},{2,3},{3,2},{4,5},{5,4},{6,7},{7,6},{8,9},{9,8},{10,11... | collective-permute-start | bytes 49160 | tf_op jit(solution)/shard_map/ppermute | solution.py:325
  24.4 41.5 %copy-start = (bf16[5,64,128]{2,1,0:T(8,128)(2,1)}, bf16[5,64,128]{2,1,0:T(8,128)(2,1)S(1)}, u32[]{:S(2)}) copy-start(bf16[5,64,128]{2,1,0:T(8,128)(2,1)S(1)} %collective-permute-done.other_ref) | copy-start | bytes 245764
  24.4 54.9 %copy-start.4 = (f32[2,128]{1,0:T(2,128)S(1)}, f32[2,128]{1,0:T(2,128)}, u32[]{:S(2)}) copy-start(f32[2,128]{1,0:T(2,128)} %gain_ref.1) | copy-start | bytes 3076
  24.4 54.9 %copy-start.5 = (f32[2,128]{1,0:T(2,128)S(1)}, f32[2,128]{1,0:T(2,128)}, u32[]{:S(2)}) copy-start(f32[2,128]{1,0:T(2,128)} %shift_ref.1) | copy-start | bytes 3076
  24.4 55.8 %copy-start.2 = (s32[8,512]{1,0:T(8,128)S(1)}, s32[8,512]{1,0:T(8,128)}, u32[]{:S(2)}) copy-start(s32[8,512]{1,0:T(8,128)} %param.13) | copy-start | bytes 49156
  65.9 15.6 %copy-start.3 = (bf16[64,128]{1,0:T(8,128)(2,1)S(1)}, bf16[64,128]{1,0:T(8,128)(2,1)}, u32[]{:S(2)}) copy-start(bf16[64,128]{1,0:T(8,128)(2,1)} %param.18) | copy-start | bytes 49156
  65.9 89.4 %all-to-all-start.1 = ((bf16[32,4,8,512]{3,2,1,0:T(8,128)(2,1)}), bf16[32,4,8,512]{3,2,1,0:T(8,128)(2,1)S(1)}, u32[]{:S(2)}, u32[]{:S(2)}) async-start(bf16[32,4,8,512]{3,2,1,0:T(8,128)(2,1)} %right.1), calls=%async_computation.1 | async-start | bytes 2097152 | tf_op jit(solution)/shard_map/all_to_all | solution.py:321
  155.3 87.3 %copy-start.1 = (bf16[32,4,8,512]{3,2,1,0:T(8,128)(2,1)}, bf16[32,4,8,512]{3,2,1,0:T(8,128)(2,1)S(1)}, u32[]{:S(2)}) copy-start(bf16[32,4,8,512]{3,2,1,0:T(8,128)(2,1)S(1)} %all-to-all-done.1.right_ref) | copy-start | bytes 3145732
  155.3 87.3 %all-to-all-start = ((bf16[32,4,8,512]{3,2,1,0:T(8,128)(2,1)}), bf16[32,4,8,512]{3,2,1,0:T(8,128)(2,1)S(1)}, u32[]{:S(2)}, u32[]{:S(2)}) async-start(bf16[32,4,8,512]{3,2,1,0:T(8,128)(2,1)} %left.1), calls=%async_computation | async-start | bytes 2097152 | tf_op jit(solution)/shard_map/all_to_all | solution.py:321
  169.9 72.8 %collective-permute-start.2 = (bf16[32,4,8,512]{3,2,1,0:T(8,128)(2,1)S(1)}, bf16[32,4,8,512]{3,2,1,0:T(8,128)(2,1)S(1)}, u32[]{:S(2)}, u32[]{:S(2)}) collective-permute-start(bf16[32,4,8,512]{3,2,1,0:T(8,128)(2,1)S(1)} %all-to-all-done.1.right_ref), channel_id=1, source_target_pairs={{0,1},{1,0},{2,3},{3,2},{4,5},{5,4},{6,7},{7,6},{8,9},{9,8},{10,11... | collective-permute-start | bytes 3145736 | tf_op jit(solution)/shard_map/ppermute | solution.py:338
  245.7 10.3 %copy-start.6 = (f32[64]{0:T(128)S(1)}, f32[64]{0:T(128)}, u32[]{:S(2)}) copy-start(f32[64]{0:T(128)} %param.21) | copy-start | bytes 772
  245.7 84.0 %all-to-all-start.2 = ((bf16[32,4,8,512]{3,2,1,0:T(8,128)(2,1)}), bf16[32,4,8,512]{3,2,1,0:T(8,128)(2,1)S(1)}, u32[]{:S(2)}, u32[]{:S(2)}) async-start(bf16[32,4,8,512]{3,2,1,0:T(8,128)(2,1)} %triangle.1), calls=%async_computation.2 | async-start | bytes 2097152 | tf_op jit(solution)/shard_map/all_to_all | solution.py:321
  382.0 1.9 collective-permute-start.3
